TPU v7x, 512 devices: a whole 4x4x16 slice. The times are simulated.
512 devices in a mesh: depth: 32 (over y, x, core), tile: 16 (over z).
Axes of the slice: x: 4, y: 4, z: 16, core: 2. Of those that a mesh axis runs over, the one named last changes fastest.
Arguments:
- field: float32 [128, 1536, 1024], P('depth', 'tile'), may hold values from -6 to 6
Outputs:
- image: float32 [4, 1536, 1024], P(None, ('tile', 'depth'))
All inputs are finite; a program needn't handle non-finite values.
Results may differ from a plain program's by a relative error of at most 0.0003.
Values sent between devices are 32-bit elements; how exact they have to be, the bound alone decides.
No kernel may reach another device: no remote copies, remote signals or barrier semaphores. Data moves between devices by JAX's collectives and lax.ppermute only.
A program may use at most 64 MiB of HBM per device.

v0:
```python
import jax
import jax.numpy as jnp
from jax import lax
from jax.sharding import PartitionSpec as P

centres = (-1.2, 0.3, 1.5)
spreads = (0.25, 0.35, 0.3)
heights = (2.0, 1.0, 3.0)
floor_density = 0.05
light_cols = 0.48
light_rows = 0.6
light_depth = 0.64


def from_behind(block, axis, distance):
    devices = range(lax.axis_size(axis))
    route = [(i - distance, i) for i in devices if i - distance in devices]
    return lax.ppermute(block, axis, route)


def extended(cells, sides, width):
    for axis, dim in sides:
        count = lax.axis_size(axis)
        ends = count - 1
        head = lax.slice_in_dim(cells, 0, width, axis=dim)
        tail = lax.slice_in_dim(cells, cells.shape[dim] - width, cells.shape[dim], axis=dim)
        cells = jnp.concatenate(
            [
                lax.ppermute(tail, axis, [(i, (i + 1) % count) for i in range(ends)]),
                cells,
                lax.ppermute(head, axis, [((i + 1) % count, i) for i in range(ends)]),
            ],
            axis=dim,
        )
    return cells


def emission(sample, slope_cols, slope_rows, slope_depth):
    density = floor_density + jnp.zeros_like(sample)
    for centre, spread, bump_height in zip(centres, spreads, heights):
        scaled = (sample - centre) / spread
        density = density + bump_height * jnp.exp(-scaled * scaled)
    facing = light_cols * slope_cols + light_rows * slope_rows + light_depth * slope_depth
    length = slope_cols * slope_cols + slope_rows * slope_rows + slope_depth * slope_depth + 1.0
    shading = 0.3 + 0.7 * jnp.abs(facing) * lax.rsqrt(length)
    colour = jnp.stack(
        [
            shading * jax.nn.sigmoid(2.0 * sample),
            shading * jnp.exp(-sample * sample),
            shading * jax.nn.sigmoid(-2.0 * sample),
        ]
    )
    return (density, colour)


def integrate(density, colour, spacing):
    optics = spacing * density
    running = jnp.cumsum(optics, axis=0)
    before = jnp.concatenate([jnp.zeros_like(optics[:1]), running[:-1]], axis=0)
    weight = jnp.exp(-before) * -jnp.expm1(-optics)
    return (jnp.sum(weight[None] * colour, axis=1), jnp.exp(-running[-1]))


def blend_all(pieces):
    colour_in, through_in = pieces
    passed = jnp.cumprod(through_in, axis=1)
    before = jnp.concatenate([jnp.ones_like(through_in[:, :1]), passed[:, :-1]], axis=1)
    return (jnp.sum(before * colour_in, axis=1), passed[:, -1])


def local(field):
    planes, row_count, col_count = field.shape
    depth_count = lax.axis_size("depth")
    spacing = 3.0 / (planes * depth_count)
    following = from_behind(field[:1], "depth", -1)
    further = jnp.concatenate([field[1:], following], axis=0)
    sample = 0.5 * (field + further)
    slope_depth = further - field
    edge_rows = jnp.concatenate([sample[:, :1], sample[:, -1:]], axis=1)
    edge_padded = extended(edge_rows, (("tile", 1),), 1)
    padded = jnp.concatenate([edge_padded[:, :1], sample, edge_padded[:, -1:]], axis=1)
    slope_rows = 0.5 * (padded[:, 2:] - padded[:, :-2])
    zero_col = jnp.zeros_like(sample[..., :1])
    slope_cols = 0.5 * (
        jnp.concatenate([sample[..., 1:], zero_col], axis=-1)
        - jnp.concatenate([zero_col, sample[..., :-1]], axis=-1)
    )
    density, colour = emission(sample, slope_cols, slope_rows, slope_depth)
    colour_sum, through = integrate(density, colour, spacing)
    row_share = row_count // depth_count
    colour_parts = colour_sum.reshape(3, depth_count, row_share, col_count)
    through_parts = through.reshape(1, depth_count, row_share, col_count)
    colour_out, through_out = blend_all(
        (
            lax.all_to_all(colour_parts, "depth", split_axis=1, concat_axis=1, tiled=True),
            lax.all_to_all(through_parts, "depth", split_axis=1, concat_axis=1, tiled=True),
        )
    )
    return jnp.concatenate([colour_out, 1.0 - through_out], axis=0)


def solution(mesh):
    return jax.shard_map(
        local,
        mesh=mesh,
        in_specs=(P("depth", "tile", None),),
        out_specs=P(None, ("tile", "depth"), None),
        check_vma=False,
    )
```

profile of v0, /device:TPU:96, one launch (start us, length us, event | category | flops | bytes accessed | tf_op | source)
XLA Modules:
  0.0 78.3 jit_solution(17771362351667191256)
XLA Ops:
  0.0 0.0 copy-start
  0.0 1.1 %slice.39 = f32[1,96,1024]{2,1,0:T(8,128)S(1)} slice(f32[4,96,1024]{2,1,0:T(8,128)} %param.1), slice={[0:1], [0:96], [0:1024]} | slice | bytes 786432 | tf_op jit(solution)/shard_map/slice | solution.py:75
  1.1 1.3 %collective-permute-start = (f32[1,96,1024]{2,1,0:T(8,128)S(1)}, f32[1,96,1024]{2,1,0:T(8,128)S(1)}, u32[]{:S(2)}, u32[]{:S(2)}) collective-permute-start(f32[1,96,1024]{2,1,0:T(8,128)S(1)} %slice.39), channel_id=1, source_target_pairs={{16,0},{32,16},{48,32},{64,48},{80,64},{96,80},{112,96},{128,112},... | collective-permute-start | bytes 1179656 | tf_op jit(solution)/shard_map/ppermute | solution.py:18
  2.4 1.4 %slice.38 = f32[3,96,1024]{2,1,0:T(8,128)S(1)} slice(f32[4,96,1024]{2,1,0:T(8,128)} %param.1), slice={[1:4], [0:96], [0:1024]} | slice | bytes 2359296 | tf_op jit(solution)/shard_map/slice | solution.py:76
  3.8 0.0 copy-start.1
  3.8 1.0 %collective-permute-done = f32[1,96,1024]{2,1,0:T(8,128)S(1)} collective-permute-done((f32[1,96,1024]{2,1,0:T(8,128)S(1)}, f32[1,96,1024]{2,1,0:T(8,128)S(1)}, u32[]{:S(2)}, u32[]{:S(2)}) %collective-permute-start) | collective-permute-done | bytes 393248 | tf_op jit(solution)/shard_map/ppermute | solution.py:18
  4.8 0.0 copy-done
  4.8 0.3 broadcast_multiply_fusion
  5.1 0.0 copy-done.1
  5.1 2.3 %fusion.22 = (f32[4,96,1023]{2,1,0:T(8,128)}, f32[4,96,1023]{2,1,0:T(8,128)}) fusion(f32[4,96,1024]{2,1,0:T(8,128)S(1)} %get-tuple-element.7), kind=kLoop, calls=%fused_computation.38 | loop fusion | bytes 6285312 | tf_op jit(solution)/shard_map/slice | solution.py:85
  7.4 0.6 fusion.23
  8.0 2.0 %collective-permute-start.1 = (f32[4,1,1024]{2,1,0:T(1,128)}, f32[4,1,1024]{2,1,0:T(1,128)S(1)}, u32[]{:S(2)}, u32[]{:S(2)}) collective-permute-start(f32[4,1,1024]{2,1,0:T(1,128)} %get-tuple-element.14), channel_id=1, source_target_pairs={{1,0},{2,1},{3,2},{4,3},{5,4},{6,5},{7,6},{8,7},{9,8},{10,9},{11,1... | collective-permute-start | bytes 49160 | tf_op jit(solution)/shard_map/ppermute | solution.py:31
  10.0 5.0 %collective-permute-start.2 = (f32[4,1,1024]{2,1,0:T(1,128)}, f32[4,1,1024]{2,1,0:T(1,128)}, u32[]{:S(2)}, u32[]{:S(2)}) collective-permute-start(f32[4,1,1024]{2,1,0:T(1,128)} %get-tuple-element.15), channel_id=1, source_target_pairs={{0,1},{1,2},{2,3},{3,4},{4,5},{5,6},{6,7},{7,8},{8,9},{9,10},{10,1... | collective-permute-start | bytes 49160 | tf_op jit(solution)/shard_map/ppermute | solution.py:29
  15.1 1.5 %fusion.19 = f32[4,96,1024]{2,1,0:T(8,128)S(1)} fusion(f32[4,96,1024]{2,1,0:T(8,128)S(1)} %get-tuple-element.8), kind=kOutput, calls=%fused_computation.37 | output fusion | flops 8650752 | bytes 3145728 | tf_op jit(solution)/shard_map/jit(cumsum)/reduce_window_sum | solution.py:58
  16.6 0.8 %fusion.17 = f32[1,96,1024]{2,1,0:T(8,128)} fusion(f32[4,96,1024]{2,1,0:T(8,128)S(1)} %fusion.19), kind=kLoop, calls=%fused_computation.33 | loop fusion | flops 98304 | bytes 786432 | tf_op jit(solution)/shard_map/exp | solution.py:61
  17.4 1.1 %slice.52 = f32[3,96,1024]{2,1,0:T(8,128)} slice(f32[4,96,1024]{2,1,0:T(8,128)S(1)} %fusion.19), slice={[0:3], [0:96], [0:1024]} | slice | bytes 2359296 | tf_op jit(solution)/shard_map/slice | solution.py:59
  18.5 2.2 %exp.38 = f32[1,32,3,1024]{3,0,2,1:T(1,128)} reshape(f32[1,96,1024]{2,1,0:T(8,128)} %fusion.17) | data formatting | bytes 786432 | tf_op jit(solution)/shard_map/exp | solution.py:61
  20.7 13.8 %all-to-all-start = ((f32[1,32,3,1024]{3,0,2,1:T(1,128)}), f32[1,32,3,1024]{3,0,2,1:T(1,128)}, u32[]{:S(2)}, u32[]{:S(2)}) async-start(f32[1,32,3,1024]{3,0,2,1:T(1,128)} %exp.38), calls=%async_computation | async-start | bytes 786432 | tf_op jit(solution)/shard_map/all_to_all | solution.py:96
  34.5 0.0 collective-permute-done.1
  34.5 0.0 collective-permute-done.2
  34.6 0.0 copy-start.2
  34.6 4.0 %multiply_bitcast_fusion.1 = (f32[1,4,96,1024]{3,2,1,0:T(8,128)S(1)}, f32[4,96,1024]{2,1,0:T(8,128)S(1)}) fusion(f32[4,96,1024]{2,1,0:T(8,128)S(1)} %get-tuple-element.8, f32[4,96,1024]{2,1,0:T(8,128)} %param.1, f32[1,96,1024]{2,1,0:T(8,128)S(1)} %collective-permute-done, f32[3,96,1024]{2,1,0:T(8,128)} %copy-done.1, f32[4,96,1024]{2,1,0:T(8,128)S(1)} %get-tuple-element.7, ...), kind=kLoop, calls=%fused_computation.24 | loop fusion | flops 10616832 | bytes 12612608 | tf_op jit(solution)/shard_map/stack | solution.py:46
  38.5 0.0 copy-done.2
  38.5 2.4 %fusion.12 = (f32[1,4,96,1024]{3,2,1,0:T(8,128)S(1)}, f32[1,4,96,1024]{3,2,1,0:T(8,128)S(1)}, f32[4,96,1024]{2,1,0:T(8,128)S(1)}) fusion(f32[4,96,1024]{2,1,0:T(8,128)S(1)} %get-tuple-element.6, f32[4,96,1024]{2,1,0:T(8,128)S(1)} %get-tuple-element.8, f32[3,96,1024]{2,1,0:T(8,128)S(1)} %copy-done.2), kind=kLoop, calls=%fused_computation.17 | loop fusion | flops 12189696 | bytes 9043968 | tf_op jit(solution)/shard_map/stack | solution.py:46
  40.9 1.9 %fusion = f32[3,96,1024]{2,1,0:T(8,128)} fusion(f32[1,4,96,1024]{3,2,1,0:T(8,128)S(1)} %get-tuple-element.10, f32[1,4,96,1024]{3,2,1,0:T(8,128)S(1)} %get-tuple-element.9, f32[1,4,96,1024]{3,2,1,0:T(8,128)S(1)} %get-tuple-element.5, f32[4,96,1024]{2,1,0:T(8,128)S(1)} %get-tuple-element.11), kind=kLoop, calls=%fused_computation.1 | loop fusion | flops 4423680 | bytes 7471104 | tf_op jit(solution)/shard_map/reduce_sum | solution.py:61
  42.8 1.6 %reshape.34 = f32[3,32,3,1024]{3,2,1,0:T(4,128)S(1)} reshape(f32[3,96,1024]{2,1,0:T(8,128)} %fusion) | data formatting | bytes 2359296 | tf_op jit(solution)/shard_map/reshape | solution.py:91
  44.4 1.5 %copy.6 = f32[3,32,3,1024]{3,2,0,1:T(4,128)} copy(f32[3,32,3,1024]{3,2,1,0:T(4,128)S(1)} %reshape.34) | data formatting | bytes 2359296 | tf_op jit(solution)/shard_map/reshape | solution.py:91
  45.8 0.0 all-to-all-done
  45.8 7.3 %all-to-all-start.1 = ((f32[3,32,3,1024]{3,2,0,1:T(4,128)}), f32[3,32,3,1024]{3,2,0,1:T(4,128)S(1)}, u32[]{:S(2)}, u32[]{:S(2)}) async-start(f32[3,32,3,1024]{3,2,0,1:T(4,128)} %copy.6), calls=%async_computation.1 | async-start | bytes 3145728 | tf_op jit(solution)/shard_map/all_to_all | solution.py:95
  53.2 1.1 %fusion.15 = f32[1,32,3,1024]{3,2,1,0:T(4,128)S(1)} fusion(f32[1,32,3,1024]{3,0,2,1:T(1,128)} %all-to-all-done), kind=kOutput, calls=%fused_computation.29 | output fusion | flops 3047424 | bytes 786432 | tf_op jit(solution)/shard_map/jit(cumprod)/reduce_window | solution.py:66
  54.3 0.1 slice.51
  54.4 0.1 pad_bitcast_fusion
  54.6 22.5 %all-to-all-done.1 = f32[3,32,3,1024]{3,2,0,1:T(4,128)S(1)} async-done(((f32[3,32,3,1024]{3,2,0,1:T(4,128)}), f32[3,32,3,1024]{3,2,0,1:T(4,128)S(1)}, u32[]{:S(2)}, u32[]{:S(2)}) %all-to-all-start.1) | async-done | bytes 1179680 | tf_op jit(solution)/shard_map/all_to_all | solution.py:95
  77.1 0.5 multiply_reduce_fusion
  77.6 0.7 copy.8
  (2 shorter events, 0.0 us)
Async XLA Ops:
  0.0 4.8 %copy-start = (f32[4,96,1024]{2,1,0:T(8,128)S(1)}, f32[4,96,1024]{2,1,0:T(8,128)}, u32[]{:S(2)}) copy-start(f32[4,96,1024]{2,1,0:T(8,128)} %param.1) | copy-start | bytes 4718596
  1.1 3.6 %collective-permute-start = (f32[1,96,1024]{2,1,0:T(8,128)S(1)}, f32[1,96,1024]{2,1,0:T(8,128)S(1)}, u32[]{:S(2)}, u32[]{:S(2)}) collective-permute-start(f32[1,96,1024]{2,1,0:T(8,128)S(1)} %slice.39), channel_id=1, source_target_pairs={{16,0},{32,16},{48,32},{64,48},{80,64},{96,80},{112,96},{128,112},... | collective-permute-start | bytes 1179656 | tf_op jit(solution)/shard_map/ppermute | solution.py:18
  3.8 1.3 %copy-start.1 = (f32[3,96,1024]{2,1,0:T(8,128)}, f32[3,96,1024]{2,1,0:T(8,128)S(1)}, u32[]{:S(2)}) copy-start(f32[3,96,1024]{2,1,0:T(8,128)S(1)} %slice.38) | copy-start | bytes 3538948
  8.0 26.5 %collective-permute-start.1 = (f32[4,1,1024]{2,1,0:T(1,128)}, f32[4,1,1024]{2,1,0:T(1,128)S(1)}, u32[]{:S(2)}, u32[]{:S(2)}) collective-permute-start(f32[4,1,1024]{2,1,0:T(1,128)} %get-tuple-element.14), channel_id=1, source_target_pairs={{1,0},{2,1},{3,2},{4,3},{5,4},{6,5},{7,6},{8,7},{9,8},{10,9},{11,1... | collective-permute-start | bytes 49160 | tf_op jit(solution)/shard_map/ppermute | solution.py:31
  10.0 24.5 %collective-permute-start.2 = (f32[4,1,1024]{2,1,0:T(1,128)}, f32[4,1,1024]{2,1,0:T(1,128)}, u32[]{:S(2)}, u32[]{:S(2)}) collective-permute-start(f32[4,1,1024]{2,1,0:T(1,128)} %get-tuple-element.15), channel_id=1, source_target_pairs={{0,1},{1,2},{2,3},{3,4},{4,5},{5,6},{6,7},{7,8},{8,9},{9,10},{10,1... | collective-permute-start | bytes 49160 | tf_op jit(solution)/shard_map/ppermute | solution.py:29
  20.7 25.1 %all-to-all-start = ((f32[1,32,3,1024]{3,0,2,1:T(1,128)}), f32[1,32,3,1024]{3,0,2,1:T(1,128)}, u32[]{:S(2)}, u32[]{:S(2)}) async-start(f32[1,32,3,1024]{3,0,2,1:T(1,128)} %exp.38), calls=%async_computation | async-start | bytes 786432 | tf_op jit(solution)/shard_map/all_to_all | solution.py:96
  34.6 4.0 %copy-start.2 = (f32[3,96,1024]{2,1,0:T(8,128)S(1)}, f32[3,96,1024]{2,1,0:T(8,128)}, u32[]{:S(2)}) copy-start(f32[3,96,1024]{2,1,0:T(8,128)} %slice.52) | copy-start | bytes 3538948
  45.8 31.2 %all-to-all-start.1 = ((f32[3,32,3,1024]{3,2,0,1:T(4,128)}), f32[3,32,3,1024]{3,2,0,1:T(4,128)S(1)}, u32[]{:S(2)}, u32[]{:S(2)}) async-start(f32[3,32,3,1024]{3,2,0,1:T(4,128)} %copy.6), calls=%async_computation.1 | async-start | bytes 3145728 | tf_op jit(solution)/shard_map/all_to_all | solution.py:95
where the time goes:
time: 78.7 us; the launch traced here: 78.3 us
  starting transfers between devices  29.5 us (37%)
  waiting for transfers between devices  23.5 us (30%)
  local copies, waits for them, and re-layouts  12.6 us (16%)
  other arithmetic  12.5 us (16%)
    all_to_all x1, waiting for transfers between devices, local(): lax.all_to_all(colour_parts, 'depth', split_axis=1, concat_axis=1, tiled=...  22.5 us
    all_to_all x1, starting transfers between devices, local(): lax.all_to_all(through_parts, 'depth', split_axis=1, concat_axis=1, tiled...  13.8 us
    all_to_all x1, starting transfers between devices, local(): lax.all_to_all(colour_parts, 'depth', split_axis=1, concat_axis=1, tiled=...  7.32 us
    another operation x2, other arithmetic, emission(): jnp.stack([shading * jax.nn.sigmoid(2.0 * sample), shading * jnp.exp(-sam...  6.33 us
    ppermute x1, starting transfers between devices, extended(): lax.ppermute(tail, axis, [(i, (i + 1) % count) for i in range(ends)])  5.04 us
    reshape x2, local copies, waits for them, and re-layouts, local(): colour_parts = colour_sum.reshape(3, depth_count, row_share, col_count)  3.05 us
    slice x1, local copies, waits for them, and re-layouts, local(): sample[..., 1:]  2.26 us
    exp x1, local copies, waits for them, and re-layouts, integrate(): return (jnp.sum(weight[None] * colour, axis=1), jnp.exp(-running[-1]))  2.22 us
  transfers between devices with their start and end apart: 5, of which 2 were waited for; matrix products, arithmetic and copies ran while one was open for 25% of the time, Pallas kernels for 0%

commit v1 on v0

v1 whole, which is shorter than its diff:
```python
import functools
import math

import jax
import jax.numpy as jnp
from jax import lax
from jax.experimental import pallas as pl
from jax.experimental.pallas import tpu as pltpu
from jax.sharding import PartitionSpec as P

centres = (-1.2, 0.3, 1.5)
spreads = (0.25, 0.35, 0.3)
heights = (2.0, 1.0, 3.0)
floor_density = 0.05
light_cols = 0.48
light_rows = 0.6
light_depth = 0.64

LANES = 128
LOG2E = math.log2(math.e)
FIRST = 8


def sample_step(spacing, state, low, high, half, above, below, slope_cols):
    run, through, total, tilt, middle = state
    run = run - spacing * LOG2E * floor_density
    for centre, spread, bump in zip(centres, spreads, heights):
        offset = half - 0.5 * centre
        run = run - jnp.exp2(
            (offset * offset) * (-4.0 * LOG2E / (spread * spread)) + math.log2(bump * spacing * LOG2E)
        )
    now = jnp.exp2(run)
    weight = through - now
    slope_rows = below - above
    slope_depth = high - low
    facing = (0.7 * light_cols) * slope_cols + (0.7 * light_rows) * slope_rows + (0.7 * light_depth) * slope_depth
    length = slope_cols * slope_cols + slope_rows * slope_rows + slope_depth * slope_depth + 1.0
    lit = weight * (0.3 + jnp.abs(facing) * lax.rsqrt(length))
    total = total + lit
    tilt = tilt + lit * jnp.tanh(2.0 * half)
    middle = middle + lit * jnp.exp2((half * half) * (-4.0 * LOG2E))
    return run, now, total, tilt, middle


def render_kernel(spacing, own, partner, behind, edge, corner, out, buf, cols, sems):
    planes, rows, width = own.shape
    tiles = width // LANES
    core = lax.rem(lax.axis_index("depth"), 2)
    copies = []
    for tile in range(tiles):
        lanes = pl.ds(tile * LANES, LANES)
        for ref, slot, count in ((own, core * planes, planes), (partner, (1 - core) * planes, planes), (behind, 2 * planes, 1)):
            copies.append(
                pltpu.make_async_copy(
                    ref.at[:, :, lanes], buf.at[pl.ds(slot, count), tile, pl.ds(FIRST, rows), :], sems.at[len(copies)]
                )
            )
    for copy in copies:
        copy.start()
    for plane in range(2 * planes + 1):
        for tile in range(tiles):
            lanes = slice(tile * LANES, (tile + 1) * LANES)
            row = edge[plane : plane + 1, lanes] if plane < 2 * planes else corner[:, lanes]
            buf[plane, tile, FIRST - 1 : FIRST, :] = row
            buf[plane, tile, FIRST + rows : FIRST + rows + 1, :] = row
    for copy in copies:
        copy.wait()

    samples = 2 * planes
    groups = rows // 48
    lane = lax.broadcasted_iota(jnp.int32, (8, LANES), 1)
    leftmost, rightmost = lane == 0, lane == LANES - 1

    def picked(plane, tile, group, offset):
        return buf[plane, tile, pl.ds(FIRST + 48 * group + 3 * core + offset, 8, stride=6), :]

    def column_slopes(index, carry):
        group, row = index // 3, lax.rem(index, 3)
        before = [picked(0, tile, group, row) for tile in range(tiles)]
        for plane in range(samples):
            after = [picked(plane + 1, tile, group, row) for tile in range(tiles)]
            half = [0.25 * (a + b) for a, b in zip(before, after)]
            right = [pltpu.roll(h, LANES - 1, 1) for h in half]
            left = [pltpu.roll(h, 1, 1) for h in half]
            zero = jnp.zeros_like(half[0])
            for tile in range(tiles):
                upper = jnp.where(rightmost, right[tile + 1] if tile + 1 < tiles else zero, right[tile])
                lower = jnp.where(leftmost, left[tile - 1] if tile else zero, left[tile])
                cols[plane, index, pl.ds(tile * 8, 8), :] = upper - lower
            before = after
        return carry

    lax.fori_loop(0, 3 * groups, column_slopes, 0)

    def shade(index, carry):
        group, tile = index // tiles, lax.rem(index, tiles)
        low = [picked(0, tile, group, offset) for offset in range(-1, 4)]
        zero = jnp.zeros((8, LANES), jnp.float32)
        states = [(zero, zero + 1.0, zero, zero, zero)] * 3
        for plane in range(samples):
            high = [picked(plane + 1, tile, group, offset) for offset in range(-1, 4)]
            half = [0.25 * (a + b) for a, b in zip(low, high)]
            for row in range(3):
                states[row] = sample_step(
                    spacing,
                    states[row],
                    low[row + 1],
                    high[row + 1],
                    half[row + 1],
                    half[row],
                    half[row + 2],
                    cols[plane, group * 3 + row, pl.ds(tile * 8, 8), :],
                )
            low = high
        for row in range(3):
            run, through, total, tilt, middle = states[row]
            values = (0.5 * (total + tilt), middle, 0.5 * (total - tilt), through)
            for channel, value in enumerate(values):
                start = group * 768 + row * 32 + channel * 8 + tile
                out[pl.ds(start, 8, stride=96), :] = value
        return carry

    lax.fori_loop(0, groups * tiles, shade, 0)


def blend_kernel(slabs, out):
    count = slabs.shape[0] // 96
    for row in range(3):
        through = jnp.ones((8, LANES), jnp.float32)
        colour = [jnp.zeros((8, LANES), jnp.float32)] * 3
        for slab in range(count):
            base = slab * 96 + row * 32
            for channel in range(3):
                colour[channel] = colour[channel] + through * slabs[base + channel * 8 : base + channel * 8 + 8, :]
            through = through * slabs[base + 24 : base + 32, :]
        for channel, value in enumerate((*colour, 1.0 - through)):
            for tile in range(8):
                out[row, channel : channel + 1, tile * LANES : (tile + 1) * LANES] = value[tile : tile + 1, :]


def local(field):
    planes, rows, width = field.shape
    depth = lax.axis_size("depth")
    strips = lax.axis_size("tile")
    chips = depth // 2
    spacing = 3.0 / (planes * depth)
    core = lax.rem(lax.axis_index("depth"), 2)

    partner = lax.ppermute(field, "depth", [(i, i ^ 1) for i in range(depth)])
    first = field[:1]
    behind = lax.ppermute(first, "depth", [(2 * k + 2, 2 * k) for k in range(chips - 1)])
    behind_too = lax.ppermute(first, "depth", [(2 * k + 2, 2 * k + 1) for k in range(chips - 1)])
    behind = behind + behind_too

    mine = jnp.where(core == 1, field[:, rows - 1], field[:, 0])
    theirs = jnp.where(core == 1, partner[:, rows - 1], partner[:, 0])
    edge_out = jnp.where(core == 1, jnp.concatenate([theirs, mine]), jnp.concatenate([mine, theirs]))
    beside, diagonal = [], []
    for k in range(chips):
        for t in range(strips - 1):
            upper, lower = (2 * k + 1, t), (2 * k, t + 1)
            place = lambda d, s: d * strips + s
            beside += [(place(*upper), place(*lower)), (place(*lower), place(*upper))]
            if k + 1 < chips:
                diagonal += [
                    (place(upper[0] + 2, upper[1]), place(*lower)),
                    (place(lower[0] + 2, lower[1]), place(*upper)),
                ]
    edge = lax.ppermute(edge_out, ("depth", "tile"), beside)
    corner = lax.ppermute(edge_out[:1], ("depth", "tile"), diagonal)

    parts = pl.pallas_call(
        functools.partial(render_kernel, spacing),
        out_shape=jax.ShapeDtypeStruct((chips * 96, LANES), jnp.float32),
        in_specs=[pl.BlockSpec(memory_space=pltpu.HBM)] * 3 + [pl.BlockSpec(memory_space=pltpu.VMEM)] * 2,
        out_specs=pl.BlockSpec(memory_space=pltpu.VMEM),
        scratch_shapes=[
            pltpu.VMEM((2 * planes + 1, width // LANES, rows + 16, LANES), jnp.float32),
            pltpu.VMEM((2 * planes, 6, width // LANES * 8, LANES), jnp.float32),
            pltpu.SemaphoreType.DMA((3 * (width // LANES),)),
        ],
        name="render",
    )(field, partner, behind, edge, corner)
    groups = [[2 * k + c for k in range(chips)] for c in range(2)]
    slabs = lax.all_to_all(
        parts.reshape(chips, 96, LANES), "depth", split_axis=0, concat_axis=0, tiled=True, axis_index_groups=groups
    )
    image = pl.pallas_call(
        blend_kernel,
        out_shape=jax.ShapeDtypeStruct((3, 4, width), jnp.float32),
        in_specs=[pl.BlockSpec(memory_space=pltpu.VMEM)],
        out_specs=pl.BlockSpec(memory_space=pltpu.VMEM),
        name="blend",
    )(slabs.reshape(chips * 96, LANES))
    return jnp.transpose(image, (1, 0, 2))


def solution(mesh):
    return jax.shard_map(
        local,
        mesh=mesh,
        in_specs=(P("depth", "tile", None),),
        out_specs=P(None, ("tile", "depth"), None),
        check_vma=False,
    )
```

time: 78.7 us -> 58.3 us (0.74)
  the two profiles are of different devices: /device:TPU:96 before, /device:TPU:1 now
where the time goes in v1:
time: 58.3 us; the launch traced here: 57.8 us
  blocking collectives  16.7 us (29%)
  starting transfers between devices  14.7 us (25%)
  Pallas kernels  10.3 us (18%)
  waiting for transfers between devices  7.33 us (13%)
  local copies, waits for them, and re-layouts  6.72 us (12%)
  other arithmetic  1.94 us (3%)
    all_to_all x1, blocking collectives, local(): lax.all_to_all(parts.reshape(chips, 96, LANES), 'depth', split_axis=0, co...  16.7 us
    ppermute x1, starting transfers between devices, local(): partner = lax.ppermute(field, 'depth', [(i, i ^ 1) for i in range(depth)])  8.75 us
    pallas_call x1, Pallas kernels, local(): pl.pallas_call(functools.partial(render_kernel, spacing), out_shape=jax.S...  8.53 us
    ppermute x1, waiting for transfers between devices, local(): lax.ppermute(first, 'depth', [(2 * k + 2, 2 * k + 1) for k in range(chips...  7.32 us
    unnamed x5, local copies, waits for them, and re-layouts  3.62 us
    ppermute x1, local copies, waits for them, and re-layouts, local(): partner = lax.ppermute(field, 'depth', [(i, i ^ 1) for i in range(depth)])  2.07 us
    ppermute x1, starting transfers between devices, local(): edge = lax.ppermute(edge_out, ('depth', 'tile'), beside)  1.92 us
    add x1, other arithmetic, local(): behind = behind + behind_too  1.9 us
  transfers between devices with their start and end apart: 5, of which 1 were waited for; matrix products, arithmetic and copies ran while one was open for 9% of the time, Pallas kernels for 0%

profile of v1, /device:TPU:1, one launch (start us, length us, event | category | flops | bytes accessed | tf_op | source)
XLA Modules:
  0.0 57.8 jit_solution(7348655206439223504)
XLA Ops:
  0.0 2.4 %copy.2 = f32[4,96,1024]{2,0,1:T(4,128)S(1)} copy(f32[4,96,1024]{2,1,0:T(8,128)} %own.1) | data formatting | bytes 3145728 | tf_op args[0]
  2.4 8.7 %collective-permute-start = (f32[4,96,1024]{2,0,1:T(4,128)S(1)}, f32[4,96,1024]{2,0,1:T(4,128)S(1)}, u32[]{:S(2)}, u32[]{:S(2)}) collective-permute-start(f32[4,96,1024]{2,0,1:T(4,128)S(1)} %copy.2), channel_id=1, source_target_pairs={{0,16},{16,0},{32,48},{48,32},{64,80},{80,64},{96,112},{112,96},{1... | collective-permute-start | bytes 4718600 | tf_op jit(solution)/shard_map/ppermute | solution.py:149
  11.2 1.0 %slice.18 = f32[1,96,1024]{2,1,0:T(8,128)S(1)} slice(f32[4,96,1024]{2,1,0:T(8,128)} %own.1), slice={[0:1], [0:96], [0:1024]} | slice | bytes 786432 | tf_op jit(solution)/shard_map/slice | solution.py:150
  12.2 1.4 %collective-permute-start.1 = (f32[1,96,1024]{2,1,0:T(8,128)S(1)}, f32[1,96,1024]{2,1,0:T(8,128)}, u32[]{:S(2)}, u32[]{:S(2)}) collective-permute-start(f32[1,96,1024]{2,1,0:T(8,128)S(1)} %slice.18), channel_id=1, source_target_pairs={{32,0},{64,32},{96,64},{128,96},{160,128},{192,160},{224,192},{256... | collective-permute-start | bytes 1179656 | tf_op jit(solution)/shard_map/ppermute | solution.py:151
  13.6 1.3 %collective-permute-start.2 = (f32[1,96,1024]{2,1,0:T(8,128)S(1)}, f32[1,96,1024]{2,1,0:T(8,128)}, u32[]{:S(2)}, u32[]{:S(2)}) collective-permute-start(f32[1,96,1024]{2,1,0:T(8,128)S(1)} %slice.18), channel_id=1, source_target_pairs={{32,16},{64,48},{96,80},{128,112},{160,144},{192,176},{224,208},{2... | collective-permute-start | bytes 1179656 | tf_op jit(solution)/shard_map/ppermute | solution.py:152
  14.9 0.0 collective-permute-done
  15.0 1.9 %collective-permute-start.3 = (f32[8,1024]{1,0:T(8,128)S(1)}, f32[8,1024]{1,0:T(8,128)S(1)}, u32[]{:S(2)}, u32[]{:S(2)}) collective-permute-start(f32[8,1024]{1,0:T(8,128)S(1)} %maximum_select_fusion), channel_id=1, source_target_pairs={{16,1},{1,16},{17,2},{2,17},{18,3},{3,18},{19,4},{4,19},{20,5},{5,... | collective-permute-start | bytes 98312 | tf_op jit(solution)/shard_map/ppermute | solution.py:169
  16.9 1.3 %collective-permute-start.4 = (f32[1,1024]{1,0:T(1,128)S(1)}, f32[1,1024]{1,0:T(1,128)S(1)}, u32[]{:S(2)}, u32[]{:S(2)}) collective-permute-start(f32[1,1024]{1,0:T(1,128)S(1)} %slice.28), channel_id=1, source_target_pairs={{48,1},{33,16},{49,2},{34,17},{50,3},{35,18},{51,4},{36,19},{52,5}... | collective-permute-start | bytes 12296 | tf_op jit(solution)/shard_map/ppermute | solution.py:170
  18.2 0.0 collective-permute-done.1
  18.2 7.3 %collective-permute-done.2 = f32[1,96,1024]{2,1,0:T(8,128)} collective-permute-done((f32[1,96,1024]{2,1,0:T(8,128)S(1)}, f32[1,96,1024]{2,1,0:T(8,128)}, u32[]{:S(2)}, u32[]{:S(2)}) %collective-permute-start.2) | collective-permute-done | bytes 393248 | tf_op jit(solution)/shard_map/ppermute | solution.py:152
  25.6 1.9 %add.3.behind = f32[1,96,1024]{2,1,0:T(8,128)} add(f32[1,96,1024]{2,1,0:T(8,128)} %collective-permute-done.1, f32[1,96,1024]{2,1,0:T(8,128)} %collective-permute-done.2) | non-fusion elementwise | flops 98304 | bytes 1179648 | tf_op jit(solution)/shard_map/add | solution.py:153
  27.5 2.1 %copy.5.partner = f32[4,96,1024]{2,1,0:T(8,128)} copy(f32[4,96,1024]{2,0,1:T(4,128)S(1)} %collective-permute-done) | data formatting | bytes 3145728 | tf_op jit(solution)/shard_map/ppermute | solution.py:149
  29.5 0.0 collective-permute-done.4.corner
  29.5 0.0 copy-start.1
  29.5 0.0 collective-permute-done.3.edge
  29.5 0.6 %copy-done.1 = f32[1,1024]{1,0:T(1,128)} copy-done((f32[1,1024]{1,0:T(1,128)}, f32[1,1024]{1,0:T(1,128)S(1)}, u32[]{:S(2)}) %copy-start.1) | copy-done | bytes 4120
  30.1 0.0 copy-start
  30.1 0.6 %copy-done = f32[8,1024]{1,0:T(8,128)} copy-done((f32[8,1024]{1,0:T(8,128)}, f32[8,1024]{1,0:T(8,128)S(1)}, u32[]{:S(2)}) %copy-start) | copy-done | bytes 32792
  30.7 8.5 %render.1 = f32[1536,128]{1,0:T(8,128)} custom-call(f32[4,96,1024]{2,1,0:T(8,128)} %own.1, f32[4,96,1024]{2,1,0:T(8,128)} %copy.5.partner, f32[1,96,1024]{2,1,0:T(8,128)} %add.3.behind, f32[8,1024]{1,0:T(8,128)} %copy-done, f32[1,1024]{1,0:T(1,128)} %copy-done.1), custom_call_target="tpu_custom_call" | custom-call | tf_op jit(solution)/shard_map/render/pallas_call | solution.py:172
  39.3 16.7 %all_to_all.5 = f32[16,96,128]{2,1,0:T(8,128)} all-to-all(f32[16,96,128]{2,1,0:T(8,128)} %bitcast.7), channel_id=1, replica_groups={{0,32,64,96,128,160,192,224,256,288,320,352,384,416,448,480},{16,48,80,..., dimensions={0} | all-to-all | bytes 1572864 | tf_op jit(solution)/shard_map/all_to_all | solution.py:185
  56.0 1.8 %blend.1 = f32[3,4,1024]{2,1,0:T(4,128)} custom-call(f32[1536,128]{1,0:T(8,128)} %bitcast.8), custom_call_target="tpu_custom_call" | custom-call | tf_op jit(solution)/shard_map/blend/pallas_call | solution.py:188
  (4 shorter events, 0.0 us)
Async XLA Ops:
  2.4 12.5 %collective-permute-start = (f32[4,96,1024]{2,0,1:T(4,128)S(1)}, f32[4,96,1024]{2,0,1:T(4,128)S(1)}, u32[]{:S(2)}, u32[]{:S(2)}) collective-permute-start(f32[4,96,1024]{2,0,1:T(4,128)S(1)} %copy.2), channel_id=1, source_target_pairs={{0,16},{16,0},{32,48},{48,32},{64,80},{80,64},{96,112},{112,96},{1... | collective-permute-start | bytes 4718600 | tf_op jit(solution)/shard_map/ppermute | solution.py:149
  12.2 6.0 %collective-permute-start.1 = (f32[1,96,1024]{2,1,0:T(8,128)S(1)}, f32[1,96,1024]{2,1,0:T(8,128)}, u32[]{:S(2)}, u32[]{:S(2)}) collective-permute-start(f32[1,96,1024]{2,1,0:T(8,128)S(1)} %slice.18), channel_id=1, source_target_pairs={{32,0},{64,32},{96,64},{128,96},{160,128},{192,160},{224,192},{256... | collective-permute-start | bytes 1179656 | tf_op jit(solution)/shard_map/ppermute | solution.py:151
  13.6 11.9 %collective-permute-start.2 = (f32[1,96,1024]{2,1,0:T(8,128)S(1)}, f32[1,96,1024]{2,1,0:T(8,128)}, u32[]{:S(2)}, u32[]{:S(2)}) collective-permute-start(f32[1,96,1024]{2,1,0:T(8,128)S(1)} %slice.18), channel_id=1, source_target_pairs={{32,16},{64,48},{96,80},{128,112},{160,144},{192,176},{224,208},{2... | collective-permute-start | bytes 1179656 | tf_op jit(solution)/shard_map/ppermute | solution.py:152
  15.0 14.6 %collective-permute-start.3 = (f32[8,1024]{1,0:T(8,128)S(1)}, f32[8,1024]{1,0:T(8,128)S(1)}, u32[]{:S(2)}, u32[]{:S(2)}) collective-permute-start(f32[8,1024]{1,0:T(8,128)S(1)} %maximum_select_fusion), channel_id=1, source_target_pairs={{16,1},{1,16},{17,2},{2,17},{18,3},{3,18},{19,4},{4,19},{20,5},{5,... | collective-permute-start | bytes 98312 | tf_op jit(solution)/shard_map/ppermute | solution.py:169
  16.9 12.6 %collective-permute-start.4 = (f32[1,1024]{1,0:T(1,128)S(1)}, f32[1,1024]{1,0:T(1,128)S(1)}, u32[]{:S(2)}, u32[]{:S(2)}) collective-permute-start(f32[1,1024]{1,0:T(1,128)S(1)} %slice.28), channel_id=1, source_target_pairs={{48,1},{33,16},{49,2},{34,17},{50,3},{35,18},{51,4},{36,19},{52,5}... | collective-permute-start | bytes 12296 | tf_op jit(solution)/shard_map/ppermute | solution.py:170
  29.5 0.6 %copy-start.1 = (f32[1,1024]{1,0:T(1,128)}, f32[1,1024]{1,0:T(1,128)S(1)}, u32[]{:S(2)}) copy-start(f32[1,1024]{1,0:T(1,128)S(1)} %collective-permute-done.4.corner) | copy-start | bytes 12292
  30.1 0.6 %copy-start = (f32[8,1024]{1,0:T(8,128)}, f32[8,1024]{1,0:T(8,128)S(1)}, u32[]{:S(2)}) copy-start(f32[8,1024]{1,0:T(8,128)S(1)} %collective-permute-done.3.edge) | copy-start | bytes 98308

commit v2 on v1

v2 whole, which is shorter than its diff:
```python
import functools
import math

import jax
import jax.numpy as jnp
from jax import lax
from jax.experimental import pallas as pl
from jax.experimental.pallas import tpu as pltpu
from jax.sharding import PartitionSpec as P

centres = (-1.2, 0.3, 1.5)
spreads = (0.25, 0.35, 0.3)
heights = (2.0, 1.0, 3.0)
floor_density = 0.05
light_cols = 0.48
light_rows = 0.6
light_depth = 0.64

LANES = 128
LOG2E = math.log2(math.e)
FIRST = 8
PITCH = 112
VMEM = pl.BlockSpec(memory_space=pltpu.VMEM)


def sample_step(spacing, state, low, high, half, above, below, slope_cols):
    run, through, total, tilt, middle = state
    run = run - spacing * LOG2E * floor_density
    for centre, spread, bump in zip(centres, spreads, heights):
        offset = half - 0.5 * centre
        run = run - jnp.exp2(
            (offset * offset) * (-4.0 * LOG2E / (spread * spread)) + math.log2(bump * spacing * LOG2E)
        )
    now = jnp.exp2(run)
    weight = through - now
    slope_rows = below - above
    slope_depth = high - low
    facing = (0.7 * light_cols) * slope_cols + (0.7 * light_rows) * slope_rows + (0.7 * light_depth) * slope_depth
    length = slope_cols * slope_cols + slope_rows * slope_rows + slope_depth * slope_depth + 1.0
    lit = weight * (0.3 + jnp.abs(facing) * lax.rsqrt(length))
    total = total + lit
    tilt = tilt + lit * jnp.tanh(2.0 * half)
    middle = middle + lit * jnp.exp2((half * half) * (-4.0 * LOG2E))
    return run, now, total, tilt, middle


def finished(state):
    run, through, total, tilt, middle = state
    return 0.5 * (total + tilt), middle, 0.5 * (total - tilt), through


def lane_masks():
    lane = lax.broadcasted_iota(jnp.int32, (8, LANES), 1)
    return lane == 0, lane == LANES - 1


def tile_slopes(half):
    leftmost, rightmost = lane_masks()
    right = [pltpu.roll(h, LANES - 1, 1) for h in half]
    left = [pltpu.roll(h, 1, 1) for h in half]
    zero = jnp.zeros_like(half[0])
    slopes = []
    for tile in range(len(half)):
        upper = jnp.where(rightmost, right[tile + 1] if tile + 1 < len(half) else zero, right[tile])
        lower = jnp.where(leftmost, left[tile - 1] if tile else zero, left[tile])
        slopes.append(upper - lower)
    return slopes


def row_slopes(half):
    leftmost, rightmost = lane_masks()
    tile = lax.broadcasted_iota(jnp.int32, (8, LANES), 0)
    right = pltpu.roll(half, LANES - 1, 1)
    left = pltpu.roll(half, 1, 1)
    upper = jnp.where(rightmost, jnp.where(tile == 7, 0.0, pltpu.roll(right, 7, 0)), right)
    lower = jnp.where(leftmost, jnp.where(tile == 0, 0.0, pltpu.roll(left, 1, 0)), left)
    return upper - lower


def core_index():
    return lax.rem(lax.axis_index("depth"), 2)


def fetch_kernel(field, own, front, sems):
    copies = [
        pltpu.make_async_copy(field.at[pl.ds(0, 1)], front, sems.at[0]),
        pltpu.make_async_copy(field, own, sems.at[1]),
    ]
    for copy in copies:
        copy.start()
    for copy in copies:
        copy.wait()


def edge_kernel(own, partner, edge, first, inner):
    planes, rows, width = own.shape
    core = core_index()
    for plane in range(2 * planes):
        at_core0, at_core1 = (own, partner) if plane < planes else (partner, own)
        for tile in range(width // LANES):
            lanes = slice(tile * LANES, (tile + 1) * LANES)
            at = plane * (width // LANES) + tile
            row = jnp.where(
                core == 0, at_core0[plane % planes, 0:1, lanes], at_core1[plane % planes, rows - 1 : rows, lanes]
            )
            edge[at : at + 1, :] = row
            if plane == 0:
                first[at : at + 1, :] = row
            inner[at : at + 1, :] = jnp.where(
                core == 0, at_core0[plane % planes, 1:2, lanes], at_core1[plane % planes, rows - 2 : rows - 1, lanes]
            )


def bulk_kernel(spacing, own, partner, state_out, last, buf, cols):
    planes, rows, width = own.shape
    tiles = width // LANES
    core = core_index()
    for plane in range(planes):
        for tile in range(tiles):
            lanes = slice(tile * LANES, (tile + 1) * LANES)
            buf[core * planes + plane, tile, FIRST : FIRST + rows, :] = own[plane, :, lanes]
            buf[(1 - core) * planes + plane, tile, FIRST : FIRST + rows, :] = partner[plane, :, lanes]

    samples = 2 * planes - 1
    groups = rows // 48
    last[...] = buf[samples]

    def picked(plane, tile, group, offset):
        return buf[plane, tile, pl.ds(FIRST + 48 * group + 3 * core + offset, 8, stride=6), :]

    def column_slopes(index, carry):
        group, row = index // 3, lax.rem(index, 3)
        before = [picked(0, tile, group, row) for tile in range(tiles)]
        for plane in range(samples):
            after = [picked(plane + 1, tile, group, row) for tile in range(tiles)]
            slopes = tile_slopes([0.25 * (a + b) for a, b in zip(before, after)])
            for tile in range(tiles):
                cols[plane, index, pl.ds(tile * 8, 8), :] = slopes[tile]
            before = after
        return carry

    lax.fori_loop(0, 3 * groups, column_slopes, 0)

    def shade(index, carry):
        group, tile = index // tiles, lax.rem(index, tiles)
        low = [picked(0, tile, group, offset) for offset in range(-1, 4)]
        zero = jnp.zeros((8, LANES), jnp.float32)
        states = [(zero, zero + 1.0, zero, zero, zero)] * 3
        for plane in range(samples):
            high = [picked(plane + 1, tile, group, offset) for offset in range(-1, 4)]
            half = [0.25 * (a + b) for a, b in zip(low, high)]
            for row in range(3):
                states[row] = sample_step(
                    spacing,
                    states[row],
                    low[row + 1],
                    high[row + 1],
                    half[row + 1],
                    half[row],
                    half[row + 2],
                    cols[plane, group * 3 + row, pl.ds(tile * 8, 8), :],
                )
            low = high
        for row in range(3):
            for n, value in enumerate(states[row]):
                state_out[n, group * 3 + row, pl.ds(tile * 8, 8), :] = value
        return carry

    lax.fori_loop(0, groups * tiles, shade, 0)


def rest_kernel(spacing, state, last, behind0, behind1, edge, inner, beside, corner, out, buf, cols):
    tiles = last.shape[0]
    rows = behind0.shape[1]
    groups = rows // 48
    core = core_index()

    @pl.when(core == 0)
    def _():
        for tile in range(tiles):
            buf[tile, FIRST : FIRST + rows, :] = behind0[0, :, tile * LANES : (tile + 1) * LANES]

    @pl.when(core == 1)
    def _():
        for tile in range(tiles):
            buf[tile, FIRST : FIRST + rows, :] = behind1[0, :, tile * LANES : (tile + 1) * LANES]

    def picked(ref, tile, group, offset):
        return ref[tile, pl.ds(FIRST + 48 * group + 3 * core + offset, 8, stride=6), :]

    for index in range(3 * groups):
        group, row = divmod(index, 3)
        half = [0.25 * (picked(last, tile, group, row) + picked(buf, tile, group, row)) for tile in range(tiles)]
        for tile, slope in enumerate(tile_slopes(half)):
            cols[index, tile * 8 : tile * 8 + 8, :] = slope

    def shade(index, carry):
        group, tile = index // tiles, lax.rem(index, tiles)
        low = [picked(last, tile, group, offset) for offset in range(-1, 4)]
        high = [picked(buf, tile, group, offset) for offset in range(-1, 4)]
        half = [0.25 * (a + b) for a, b in zip(low, high)]
        for row in range(3):
            values = finished(
                sample_step(
                    spacing,
                    tuple(state[n, group * 3 + row, pl.ds(tile * 8, 8), :] for n in range(5)),
                    low[row + 1],
                    high[row + 1],
                    half[row + 1],
                    half[row],
                    half[row + 2],
                    cols[group * 3 + row, pl.ds(tile * 8, 8), :],
                )
            )
            for channel, value in enumerate(values):
                out[pl.ds(group * 768 + row * 32 + channel * 8 + tile, 8, stride=96), :] = value
        return carry

    lax.fori_loop(0, groups * tiles, shade, 0)

    samples = edge.shape[0] // 8

    def stacked(offset):
        view = buf.reshape(tiles * PITCH, LANES)
        return view[pl.ds(FIRST + offset, 8, stride=PITCH), :]

    def plane_rows(plane):
        at = slice(plane * 8, plane * 8 + 8)
        if plane < samples:
            return edge[at, :], inner[at, :], beside[at, :]
        return stacked((rows - 1) * core), stacked(1 + (rows - 3) * core), corner[...]

    zero = jnp.zeros((8, LANES), jnp.float32)
    line = (zero, zero + 1.0, zero, zero, zero)
    low = plane_rows(0)
    for plane in range(samples):
        high = plane_rows(plane + 1)
        half, within, beyond = [0.25 * (a + b) for a, b in zip(low, high)]
        above = jnp.where(core == 0, beyond, within)
        below = jnp.where(core == 0, within, beyond)
        line = sample_step(spacing, line, low[0], high[0], half, above, below, row_slopes(half))
        low = high
    place = core * (out.shape[0] - 32)
    for channel, value in enumerate(finished(line)):
        out[pl.ds(pl.multiple_of(place + channel * 8, 8), 8), :] = value


def blend_kernel(slabs, out):
    count = slabs.shape[0] // 96
    for row in range(3):
        through = jnp.ones((8, LANES), jnp.float32)
        colour = [jnp.zeros((8, LANES), jnp.float32)] * 3
        for slab in range(count):
            base = slab * 96 + row * 32
            for channel in range(3):
                colour[channel] = colour[channel] + through * slabs[base + channel * 8 : base + channel * 8 + 8, :]
            through = through * slabs[base + 24 : base + 32, :]
        for channel, value in enumerate((*colour, 1.0 - through)):
            for tile in range(8):
                out[row, channel : channel + 1, tile * LANES : (tile + 1) * LANES] = value[tile : tile + 1, :]


def f32(*shape):
    return jax.ShapeDtypeStruct(shape, jnp.float32)


def cost(flops, size):
    return pl.CostEstimate(flops=flops, bytes_accessed=size, transcendentals=0)


def local(field):
    planes, rows, width = field.shape
    depth = lax.axis_size("depth")
    strips = lax.axis_size("tile")
    chips = depth // 2
    tiles = width // LANES
    spacing = 3.0 / (planes * depth)

    partner = lax.ppermute(field, "depth", [(i, i ^ 1) for i in range(depth)])
    own, front = pl.pallas_call(
        fetch_kernel,
        out_shape=(f32(*field.shape), f32(1, rows, width)),
        in_specs=[pl.BlockSpec(memory_space=pltpu.HBM)],
        out_specs=(VMEM, VMEM),
        scratch_shapes=[pltpu.SemaphoreType.DMA((2,))],
        compiler_params=pltpu.CompilerParams(vmem_limit_bytes=4 << 20),
        cost_estimate=cost(1 << 10, 1 << 22),
        name="fetch",
    )(field)
    behind0 = lax.ppermute(front, "depth", [(2 * k + 2, 2 * k) for k in range(chips - 1)])
    behind1 = lax.ppermute(front, "depth", [(2 * k + 2, 2 * k + 1) for k in range(chips - 1)])

    edge, first, inner = pl.pallas_call(
        edge_kernel,
        out_shape=(f32(2 * planes * tiles, LANES), f32(tiles, LANES), f32(2 * planes * tiles, LANES)),
        in_specs=[VMEM, VMEM],
        out_specs=(VMEM, VMEM, VMEM),
        compiler_params=pltpu.CompilerParams(vmem_limit_bytes=4 << 20),
        cost_estimate=cost(1 << 20, 1 << 19),
        name="edges",
    )(own, partner)
    across, diagonal = [], []
    place = lambda d, s: d * strips + s
    for k in range(chips):
        for t in range(strips - 1):
            upper, lower = (2 * k + 1, t), (2 * k, t + 1)
            across += [(place(*upper), place(*lower)), (place(*lower), place(*upper))]
            if k + 1 < chips:
                diagonal += [
                    (place(upper[0] + 2, upper[1]), place(*lower)),
                    (place(lower[0] + 2, lower[1]), place(*upper)),
                ]
    beside = lax.ppermute(edge, ("depth", "tile"), across)
    corner = lax.ppermute(first, ("depth", "tile"), diagonal)

    state, last = pl.pallas_call(
        functools.partial(bulk_kernel, spacing),
        out_shape=(f32(5, rows // 16, tiles * 8, LANES), f32(tiles, PITCH, LANES)),
        in_specs=[VMEM, VMEM],
        out_specs=(VMEM, VMEM),
        scratch_shapes=[
            pltpu.VMEM((2 * planes, tiles, PITCH, LANES), jnp.float32),
            pltpu.VMEM((2 * planes - 1, rows // 16, tiles * 8, LANES), jnp.float32),
        ],
        compiler_params=pltpu.CompilerParams(vmem_limit_bytes=16 << 20),
        cost_estimate=cost(1 << 27, 1 << 22),
        name="bulk",
    )(own, partner)
    parts = pl.pallas_call(
        functools.partial(rest_kernel, spacing),
        out_shape=f32(chips * 96, LANES),
        in_specs=[VMEM] * 8,
        out_specs=VMEM,
        scratch_shapes=[
            pltpu.VMEM((tiles, PITCH, LANES), jnp.float32),
            pltpu.VMEM((rows // 16, tiles * 8, LANES), jnp.float32),
        ],
        compiler_params=pltpu.CompilerParams(vmem_limit_bytes=16 << 20),
        cost_estimate=cost(1 << 24, 1 << 21),
        name="rest",
    )(state, last, behind0, behind1, edge, inner, beside, corner)
    slabs = lax.all_to_all(
        parts.reshape(chips, 96, LANES),
        "depth",
        split_axis=0,
        concat_axis=0,
        tiled=True,
        axis_index_groups=[[2 * k + c for k in range(chips)] for c in range(2)],
    )
    image = pl.pallas_call(
        blend_kernel,
        out_shape=f32(3, 4, width),
        in_specs=[VMEM],
        out_specs=VMEM,
        compiler_params=pltpu.CompilerParams(vmem_limit_bytes=8 << 20),
        name="blend",
    )(slabs.reshape(chips * 96, LANES))
    return jnp.transpose(image, (1, 0, 2))


def solution(mesh):
    return jax.shard_map(
        local,
        mesh=mesh,
        in_specs=(P("depth", "tile", None),),
        out_specs=P(None, ("tile", "depth"), None),
        check_vma=False,
    )
```

time: 58.3 us -> 45.6 us (0.78)
  the two profiles are of different devices: /device:TPU:1 before, /device:TPU:225 now
where the time goes in v2:
time: 45.6 us; the launch traced here: 45.3 us
  blocking collectives  25.2 us (55%)
  starting transfers between devices  10.5 us (23%)
  Pallas kernels  6.52 us (14%)
  waiting for transfers between devices  1.56 us (3%)
  local copies, waits for them, and re-layouts  1.4 us (3%)
    all_to_all x1, blocking collectives, local(): lax.all_to_all(parts.reshape(chips, 96, LANES), 'depth', split_axis=0, co...  25.2 us
    ppermute x1, starting transfers between devices, local(): beside = lax.ppermute(edge, ('depth', 'tile'), across)  4.65 us
    pallas_call x1, Pallas kernels, local(): pl.pallas_call(functools.partial(bulk_kernel, spacing), out_shape=(f32(5,...  4.15 us
    ppermute x1, starting transfers between devices, local(): partner = lax.ppermute(field, 'depth', [(i, i ^ 1) for i in range(depth)])  2.57 us
    ppermute x1, waiting for transfers between devices, local(): corner = lax.ppermute(first, ('depth', 'tile'), diagonal)  1.55 us
    unnamed x2, local copies, waits for them, and re-layouts  1.4 us
    pallas_call x1, Pallas kernels, local(): pl.pallas_call(functools.partial(rest_kernel, spacing), out_shape=f32(chi...  1.29 us
    ppermute x1, starting transfers between devices, local(): lax.ppermute(front, 'depth', [(2 * k + 2, 2 * k + 1) for k in range(chips...  1.29 us
  transfers between devices with their start and end apart: 5, of which 1 were waited for; matrix products, arithmetic and copies ran while one was open for 0% of the time, Pallas kernels for 10%

profile of v2, /device:TPU:225, one launch (start us, length us, event | category | flops | bytes accessed | tf_op | source)
XLA Modules:
  0.0 45.3 jit_solution(14719479079293084085)
XLA Ops:
  0.0 2.6 %collective-permute-start = (f32[4,96,1024]{2,1,0:T(8,128)}, f32[4,96,1024]{2,1,0:T(8,128)S(1)}, u32[]{:S(2)}, u32[]{:S(2)}) collective-permute-start(f32[4,96,1024]{2,1,0:T(8,128)} %field.1), channel_id=1, source_target_pairs={{0,16},{16,0},{32,48},{48,32},{64,80},{80,64},{96,112},{112,96},{1... | collective-permute-start | bytes 4718600 | tf_op jit(solution)/shard_map/ppermute | solution.py:279
  2.6 0.0 copy-start
  2.6 1.4 %copy-done = f32[4,96,1024]{2,1,0:T(8,128)S(1)} copy-done((f32[4,96,1024]{2,1,0:T(8,128)S(1)}, f32[4,96,1024]{2,1,0:T(8,128)}, u32[]{:S(2)}) %copy-start) | copy-done | bytes 1572888
  4.0 0.3 fetch.1
  4.3 1.3 %collective-permute-start.2 = (f32[1,96,1024]{2,1,0:T(8,128)S(1)}, f32[1,96,1024]{2,1,0:T(8,128)S(1)}, u32[]{:S(2)}, u32[]{:S(2)}) collective-permute-start(f32[1,96,1024]{2,1,0:T(8,128)S(1)} %get-tuple-element.15), channel_id=1, source_target_pairs={{32,16},{64,48},{96,80},{128,112},{160,144},{192,176},{224,208},{2... | collective-permute-start | bytes 1179656 | tf_op jit(solution)/shard_map/ppermute | solution.py:291
  5.6 0.7 %collective-permute-start.1 = (f32[1,96,1024]{2,1,0:T(8,128)S(1)}, f32[1,96,1024]{2,1,0:T(8,128)S(1)}, u32[]{:S(2)}, u32[]{:S(2)}) collective-permute-start(f32[1,96,1024]{2,1,0:T(8,128)S(1)} %get-tuple-element.15), channel_id=1, source_target_pairs={{32,0},{64,32},{96,64},{128,96},{160,128},{192,160},{224,192},{256... | collective-permute-start | bytes 1179656 | tf_op jit(solution)/shard_map/ppermute | solution.py:290
  6.3 0.0 collective-permute-done.partner
  6.3 0.1 edges.1
  6.4 4.7 %collective-permute-start.3 = (f32[64,128]{1,0:T(8,128)S(1)}, f32[64,128]{1,0:T(8,128)S(1)}, u32[]{:S(2)}, u32[]{:S(2)}) collective-permute-start(f32[64,128]{1,0:T(8,128)S(1)} %get-tuple-element.16.edge), channel_id=1, source_target_pairs={{16,1},{1,16},{17,2},{2,17},{18,3},{3,18},{19,4},{4,19},{20,5},{5,... | collective-permute-start | bytes 98312 | tf_op jit(solution)/shard_map/ppermute | solution.py:313
  11.1 1.3 %collective-permute-start.4 = (f32[8,128]{1,0:T(8,128)S(1)}, f32[8,128]{1,0:T(8,128)S(1)}, u32[]{:S(2)}, u32[]{:S(2)}) collective-permute-start(f32[8,128]{1,0:T(8,128)S(1)} %get-tuple-element.18), channel_id=1, source_target_pairs={{48,1},{33,16},{49,2},{34,17},{50,3},{35,18},{51,4},{36,19},{52,5}... | collective-permute-start | bytes 12296 | tf_op jit(solution)/shard_map/ppermute | solution.py:314
  12.4 4.2 %bulk.1 = (f32[5,6,64,128]{3,2,1,0:T(8,128)S(1)}, f32[8,112,128]{2,1,0:T(8,128)S(1)}) custom-call(f32[4,96,1024]{2,1,0:T(8,128)S(1)} %get-tuple-element.12.own, f32[4,96,1024]{2,1,0:T(8,128)S(1)} %collective-permute-done.partner), custom_call_target="tpu_custom_call" | custom-call | flops 134217728 | bytes 4194304 | tf_op jit(solution)/shard_map/bulk/pallas_call | solution.py:316
  16.5 0.0 collective-permute-done.2.behind1
  16.5 0.0 collective-permute-done.1.behind0
  16.5 1.6 %collective-permute-done.4.corner = f32[8,128]{1,0:T(8,128)S(1)} collective-permute-done((f32[8,128]{1,0:T(8,128)S(1)}, f32[8,128]{1,0:T(8,128)S(1)}, u32[]{:S(2)}, u32[]{:S(2)}) %collective-permute-start.4) | collective-permute-done | bytes 4128 | tf_op jit(solution)/shard_map/ppermute | solution.py:314
  18.1 0.0 collective-permute-done.3.beside
  18.1 1.3 %rest.1 = f32[1536,128]{1,0:T(8,128)S(1)} custom-call(f32[5,6,64,128]{3,2,1,0:T(8,128)S(1)} %get-tuple-element.13.state, f32[8,112,128]{2,1,0:T(8,128)S(1)} %get-tuple-element.14.last, f32[1,96,1024]{2,1,0:T(8,128)S(1)} %collective-permute-done.1.behind0, f32[1,96,1024]{2,1,0:T(8,128)S(1)} %collective-permute-done.2.behind1, ...), custom_call_target="tpu_custom_call" | custom-call | flops 16777216 | bytes 2097152 | tf_op jit(solution)/shard_map/rest/pallas_call | solution.py:329
  19.4 25.2 %all_to_all.5 = f32[16,96,128]{2,1,0:T(8,128)S(1)} all-to-all(f32[16,96,128]{2,1,0:T(8,128)S(1)} %bitcast.4), channel_id=1, replica_groups={{0,32,64,96,128,160,192,224,256,288,320,352,384,416,448,480},{16,48,80,..., dimensions={0} | all-to-all | bytes 1572864 | tf_op jit(solution)/shard_map/all_to_all | solution.py:342
  44.6 0.7 %blend.1 = f32[3,4,1024]{2,1,0:T(4,128)} custom-call(f32[1536,128]{1,0:T(8,128)S(1)} %bitcast.3), custom_call_target="tpu_custom_call" | custom-call | tf_op jit(solution)/shard_map/blend/pallas_call | solution.py:350
Async XLA Ops:
  0.0 6.3 %collective-permute-start = (f32[4,96,1024]{2,1,0:T(8,128)}, f32[4,96,1024]{2,1,0:T(8,128)S(1)}, u32[]{:S(2)}, u32[]{:S(2)}) collective-permute-start(f32[4,96,1024]{2,1,0:T(8,128)} %field.1), channel_id=1, source_target_pairs={{0,16},{16,0},{32,48},{48,32},{64,80},{80,64},{96,112},{112,96},{1... | collective-permute-start | bytes 4718600 | tf_op jit(solution)/shard_map/ppermute | solution.py:279
  2.6 1.4 %copy-start = (f32[4,96,1024]{2,1,0:T(8,128)S(1)}, f32[4,96,1024]{2,1,0:T(8,128)}, u32[]{:S(2)}) copy-start(f32[4,96,1024]{2,1,0:T(8,128)} %field.1) | copy-start | bytes 4718596
  4.3 12.2 %collective-permute-start.2 = (f32[1,96,1024]{2,1,0:T(8,128)S(1)}, f32[1,96,1024]{2,1,0:T(8,128)S(1)}, u32[]{:S(2)}, u32[]{:S(2)}) collective-permute-start(f32[1,96,1024]{2,1,0:T(8,128)S(1)} %get-tuple-element.15), channel_id=1, source_target_pairs={{32,16},{64,48},{96,80},{128,112},{160,144},{192,176},{224,208},{2... | collective-permute-start | bytes 1179656 | tf_op jit(solution)/shard_map/ppermute | solution.py:291
  5.6 10.9 %collective-permute-start.1 = (f32[1,96,1024]{2,1,0:T(8,128)S(1)}, f32[1,96,1024]{2,1,0:T(8,128)S(1)}, u32[]{:S(2)}, u32[]{:S(2)}) collective-permute-start(f32[1,96,1024]{2,1,0:T(8,128)S(1)} %get-tuple-element.15), channel_id=1, source_target_pairs={{32,0},{64,32},{96,64},{128,96},{160,128},{192,160},{224,192},{256... | collective-permute-start | bytes 1179656 | tf_op jit(solution)/shard_map/ppermute | solution.py:290
  6.4 11.7 %collective-permute-start.3 = (f32[64,128]{1,0:T(8,128)S(1)}, f32[64,128]{1,0:T(8,128)S(1)}, u32[]{:S(2)}, u32[]{:S(2)}) collective-permute-start(f32[64,128]{1,0:T(8,128)S(1)} %get-tuple-element.16.edge), channel_id=1, source_target_pairs={{16,1},{1,16},{17,2},{2,17},{18,3},{3,18},{19,4},{4,19},{20,5},{5,... | collective-permute-start | bytes 98312 | tf_op jit(solution)/shard_map/ppermute | solution.py:313
  11.1 7.0 %collective-permute-start.4 = (f32[8,128]{1,0:T(8,128)S(1)}, f32[8,128]{1,0:T(8,128)S(1)}, u32[]{:S(2)}, u32[]{:S(2)}) collective-permute-start(f32[8,128]{1,0:T(8,128)S(1)} %get-tuple-element.18), channel_id=1, source_target_pairs={{48,1},{33,16},{49,2},{34,17},{50,3},{35,18},{51,4},{36,19},{52,5}... | collective-permute-start | bytes 12296 | tf_op jit(solution)/shard_map/ppermute | solution.py:314

commit v3 on v2

--- a/solution.py
+++ b/solution.py
@@ -44,11 +44,6 @@
     return run, now, total, tilt, middle
 
 
-def finished(state):
-    run, through, total, tilt, middle = state
-    return 0.5 * (total + tilt), middle, 0.5 * (total - tilt), through
-
-
 def lane_masks():
     lane = lax.broadcasted_iota(jnp.int32, (8, LANES), 1)
     return lane == 0, lane == LANES - 1
@@ -81,18 +76,11 @@
     return lax.rem(lax.axis_index("depth"), 2)
 
 
-def fetch_kernel(field, own, front, sems):
-    copies = [
-        pltpu.make_async_copy(field.at[pl.ds(0, 1)], front, sems.at[0]),
-        pltpu.make_async_copy(field, own, sems.at[1]),
-    ]
-    for copy in copies:
-        copy.start()
-    for copy in copies:
-        copy.wait()
-
-
-def edge_kernel(own, partner, edge, first, inner):
+def outermost_kernel(field, outer):
+    outer[...] = jnp.where(core_index() == 0, field[0:1], field[field.shape[0] - 1 :])
+
+
+def edge_kernel(own, partner, edge, outer, inner):
     planes, rows, width = own.shape
     core = core_index()
     for plane in range(2 * planes):
@@ -104,14 +92,15 @@
                 core == 0, at_core0[plane % planes, 0:1, lanes], at_core1[plane % planes, rows - 1 : rows, lanes]
             )
             edge[at : at + 1, :] = row
-            if plane == 0:
-                first[at : at + 1, :] = row
             inner[at : at + 1, :] = jnp.where(
                 core == 0, at_core0[plane % planes, 1:2, lanes], at_core1[plane % planes, rows - 2 : rows - 1, lanes]
             )
-
-
-def bulk_kernel(spacing, own, partner, state_out, last, buf, cols):
+    tiles = width // LANES
+    ends = edge[0:tiles, :], edge[(2 * planes - 1) * tiles :, :]
+    outer[...] = jnp.where(core == 0, ends[1], ends[0])
+
+
+def bulk_kernel(spacing, own, partner, state_out, nearest, buf, cols):
     planes, rows, width = own.shape
     tiles = width // LANES
     core = core_index()
@@ -123,7 +112,7 @@
 
     samples = 2 * planes - 1
     groups = rows // 48
-    last[...] = buf[samples]
+    nearest[...] = buf[samples * (1 - core)]
 
     def picked(plane, tile, group, offset):
         return buf[plane, tile, pl.ds(FIRST + 48 * group + 3 * core + offset, 8, stride=6), :]
@@ -169,56 +158,98 @@
     lax.fori_loop(0, groups * tiles, shade, 0)
 
 
-def rest_kernel(spacing, state, last, behind0, behind1, edge, inner, beside, corner, out, buf, cols):
-    tiles = last.shape[0]
-    rows = behind0.shape[1]
-    groups = rows // 48
-    core = core_index()
-
-    @pl.when(core == 0)
+    @pl.when(lax.axis_index("depth") == lax.axis_size("depth") - 1)
     def _():
-        for tile in range(tiles):
-            buf[tile, FIRST : FIRST + rows, :] = behind0[0, :, tile * LANES : (tile + 1) * LANES]
-
-    @pl.when(core == 1)
-    def _():
-        for tile in range(tiles):
-            buf[tile, FIRST : FIRST + rows, :] = behind1[0, :, tile * LANES : (tile + 1) * LANES]
-
-    def picked(ref, tile, group, offset):
-        return ref[tile, pl.ds(FIRST + 48 * group + 3 * core + offset, 8, stride=6), :]
-
-    for index in range(3 * groups):
-        group, row = divmod(index, 3)
-        half = [0.25 * (picked(last, tile, group, row) + picked(buf, tile, group, row)) for tile in range(tiles)]
-        for tile, slope in enumerate(tile_slopes(half)):
-            cols[index, tile * 8 : tile * 8 + 8, :] = slope
-
-    def shade(index, carry):
-        group, tile = index // tiles, lax.rem(index, tiles)
-        low = [picked(last, tile, group, offset) for offset in range(-1, 4)]
-        high = [picked(buf, tile, group, offset) for offset in range(-1, 4)]
-        half = [0.25 * (a + b) for a, b in zip(low, high)]
-        for row in range(3):
-            values = finished(
-                sample_step(
+        def slopes_at_end(index, carry):
+            group, row = index // 3, lax.rem(index, 3)
+            slopes = tile_slopes([0.25 * picked(samples, tile, group, row) for tile in range(tiles)])
+            for tile in range(tiles):
+                cols[0, index, pl.ds(tile * 8, 8), :] = slopes[tile]
+            return carry
+
+        lax.fori_loop(0, 3 * groups, slopes_at_end, 0)
+
+        def shade_at_end(index, carry):
+            group, tile = index // tiles, lax.rem(index, tiles)
+            low = [picked(samples, tile, group, offset) for offset in range(-1, 4)]
+            half = [0.25 * a for a in low]
+            for row in range(3):
+                at = (group * 3 + row, pl.ds(tile * 8, 8))
+                state = sample_step(
                     spacing,
-                    tuple(state[n, group * 3 + row, pl.ds(tile * 8, 8), :] for n in range(5)),
+                    tuple(state_out[n, at[0], at[1], :] for n in range(5)),
                     low[row + 1],
-                    high[row + 1],
+                    jnp.zeros_like(low[0]),
                     half[row + 1],
                     half[row],
                     half[row + 2],
-                    cols[group * 3 + row, pl.ds(tile * 8, 8), :],
+                    cols[0, at[0], at[1], :],
                 )
+                for n, value in enumerate(state):
+                    state_out[n, at[0], at[1], :] = value
+            return carry
+
+        lax.fori_loop(0, groups * tiles, shade_at_end, 0)
+
+
+def start_state():
+    zero = jnp.zeros((8, LANES), jnp.float32)
+    return zero, zero + 1.0, zero, zero, zero
+
+
+def joined(core, present, bulk, outer):
+    _, bulk_through, *bulk_sums = bulk
+    _, outer_through, *outer_sums = outer
+    outer_through = jnp.where(present, outer_through, 1.0)
+    on_bulk = jnp.where(core == 0, 1.0, outer_through)
+    on_outer = jnp.where(core == 0, bulk_through, jnp.where(present, 1.0, 0.0))
+    total, tilt, middle = [on_bulk * a + on_outer * b for a, b in zip(bulk_sums, outer_sums)]
+    return 0.5 * (total + tilt), middle, 0.5 * (total - tilt), bulk_through * outer_through
+
+
+def rest_kernel(spacing, state, nearest, outer, edge, inner, beside, corner, out, buf, cols):
+    tiles = nearest.shape[0]
+    rows = outer.shape[1]
+    groups = rows // 48
+    core = core_index()
+    present = lax.axis_index("depth") != 1
+    for tile in range(tiles):
+        buf[tile, FIRST : FIRST + rows, :] = outer[0, :, tile * LANES : (tile + 1) * LANES]
+    to_high = jnp.where(core == 0, 1.0, -1.0)
+
+    def picked(ref, tile, group, offset):
+        return ref[tile, pl.ds(FIRST + 48 * group + 3 * core + offset, 8, stride=6), :]
+
+    for index in range(3 * groups):
+        group, row = divmod(index, 3)
+        half = [0.25 * (picked(nearest, tile, group, row) + picked(buf, tile, group, row)) for tile in range(tiles)]
+        for tile, slope in enumerate(tile_slopes(half)):
+            cols[index, tile * 8 : tile * 8 + 8, :] = slope
+
+    def shade(index, carry):
+        group, tile = index // tiles, lax.rem(index, tiles)
+        near = [picked(nearest, tile, group, offset) for offset in range(-1, 4)]
+        far = [picked(buf, tile, group, offset) for offset in range(-1, 4)]
+        half = [0.25 * (a + b) for a, b in zip(near, far)]
+        for row in range(3):
+            sample = sample_step(
+                spacing,
+                start_state(),
+                to_high * near[row + 1],
+                to_high * far[row + 1],
+                half[row + 1],
+                half[row],
+                half[row + 2],
+                cols[group * 3 + row, pl.ds(tile * 8, 8), :],
             )
-            for channel, value in enumerate(values):
+            bulk = tuple(state[n, group * 3 + row, pl.ds(tile * 8, 8), :] for n in range(5))
+            for channel, value in enumerate(joined(core, present, bulk, sample)):
                 out[pl.ds(group * 768 + row * 32 + channel * 8 + tile, 8, stride=96), :] = value
         return carry
 
     lax.fori_loop(0, groups * tiles, shade, 0)
 
-    samples = edge.shape[0] // 8
+    planes = edge.shape[0] // 8
 
     def stacked(offset):
         view = buf.reshape(tiles * PITCH, LANES)
@@ -226,22 +257,28 @@
 
     def plane_rows(plane):
         at = slice(plane * 8, plane * 8 + 8)
-        if plane < samples:
-            return edge[at, :], inner[at, :], beside[at, :]
-        return stacked((rows - 1) * core), stacked(1 + (rows - 3) * core), corner[...]
-
-    zero = jnp.zeros((8, LANES), jnp.float32)
-    line = (zero, zero + 1.0, zero, zero, zero)
-    low = plane_rows(0)
-    for plane in range(samples):
-        high = plane_rows(plane + 1)
+        return edge[at, :], inner[at, :], beside[at, :]
+
+    def line_step(line, low, high):
         half, within, beyond = [0.25 * (a + b) for a, b in zip(low, high)]
         above = jnp.where(core == 0, beyond, within)
         below = jnp.where(core == 0, within, beyond)
-        line = sample_step(spacing, line, low[0], high[0], half, above, below, row_slopes(half))
-        low = high
+        return sample_step(spacing, line, low[0], high[0], half, above, below, row_slopes(half))
+
+    line = start_state()
+    for plane in range(planes - 1):
+        line = line_step(line, plane_rows(plane), plane_rows(plane + 1))
+    zero = jnp.zeros((8, LANES), jnp.float32)
+    ended = line_step(line, plane_rows(planes - 1), (zero, zero, zero))
+    at_end = lax.axis_index("depth") == lax.axis_size("depth") - 1
+    line = tuple(jnp.where(at_end, a, b) for a, b in zip(ended, line))
+    far = stacked((rows - 1) * core), stacked(1 + (rows - 3) * core), corner[...]
+    near = [jnp.where(core == 0, a, b) for a, b in zip(plane_rows(planes - 1), plane_rows(0))]
+    low = [jnp.where(core == 0, a, b) for a, b in zip(near, far)]
+    high = [jnp.where(core == 0, b, a) for a, b in zip(near, far)]
+    sample = line_step(start_state(), low, high)
     place = core * (out.shape[0] - 32)
-    for channel, value in enumerate(finished(line)):
+    for channel, value in enumerate(joined(core, present, line, sample)):
         out[pl.ds(pl.multiple_of(place + channel * 8, 8), 8), :] = value
 
 
@@ -277,20 +314,22 @@
     spacing = 3.0 / (planes * depth)
 
     partner = lax.ppermute(field, "depth", [(i, i ^ 1) for i in range(depth)])
-    own, front = pl.pallas_call(
-        fetch_kernel,
-        out_shape=(f32(*field.shape), f32(1, rows, width)),
-        in_specs=[pl.BlockSpec(memory_space=pltpu.HBM)],
-        out_specs=(VMEM, VMEM),
-        scratch_shapes=[pltpu.SemaphoreType.DMA((2,))],
+    outer_out = pl.pallas_call(
+        outermost_kernel,
+        out_shape=f32(1, rows, width),
+        in_specs=[VMEM],
+        out_specs=VMEM,
         compiler_params=pltpu.CompilerParams(vmem_limit_bytes=4 << 20),
-        cost_estimate=cost(1 << 10, 1 << 22),
-        name="fetch",
+        cost_estimate=cost(1 << 10, 1 << 20),
+        name="outermost",
     )(field)
-    behind0 = lax.ppermute(front, "depth", [(2 * k + 2, 2 * k) for k in range(chips - 1)])
-    behind1 = lax.ppermute(front, "depth", [(2 * k + 2, 2 * k + 1) for k in range(chips - 1)])
-
-    edge, first, inner = pl.pallas_call(
+    outer = lax.ppermute(
+        outer_out,
+        "depth",
+        [(2 * k + 2, 2 * k) for k in range(chips - 1)] + [(2 * k + 1, 2 * k + 3) for k in range(chips - 1)],
+    )
+
+    edge, corner_out, inner = pl.pallas_call(
         edge_kernel,
         out_shape=(f32(2 * planes * tiles, LANES), f32(tiles, LANES), f32(2 * planes * tiles, LANES)),
         in_specs=[VMEM, VMEM],
@@ -298,7 +337,7 @@
         compiler_params=pltpu.CompilerParams(vmem_limit_bytes=4 << 20),
         cost_estimate=cost(1 << 20, 1 << 19),
         name="edges",
-    )(own, partner)
+    )(field, partner)
     across, diagonal = [], []
     place = lambda d, s: d * strips + s
     for k in range(chips):
@@ -306,14 +345,13 @@
             upper, lower = (2 * k + 1, t), (2 * k, t + 1)
             across += [(place(*upper), place(*lower)), (place(*lower), place(*upper))]
             if k + 1 < chips:
-                diagonal += [
-                    (place(upper[0] + 2, upper[1]), place(*lower)),
-                    (place(lower[0] + 2, lower[1]), place(*upper)),
-                ]
+                diagonal.append((place(2 * (k + 1) + 1, t), place(*lower)))
+            if k:
+                diagonal.append((place(2 * (k - 1), t + 1), place(*upper)))
     beside = lax.ppermute(edge, ("depth", "tile"), across)
-    corner = lax.ppermute(first, ("depth", "tile"), diagonal)
-
-    state, last = pl.pallas_call(
+    corner = lax.ppermute(corner_out, ("depth", "tile"), diagonal)
+
+    state, nearest = pl.pallas_call(
         functools.partial(bulk_kernel, spacing),
         out_shape=(f32(5, rows // 16, tiles * 8, LANES), f32(tiles, PITCH, LANES)),
         in_specs=[VMEM, VMEM],
@@ -325,11 +363,11 @@
         compiler_params=pltpu.CompilerParams(vmem_limit_bytes=16 << 20),
         cost_estimate=cost(1 << 27, 1 << 22),
         name="bulk",
-    )(own, partner)
+    )(field, partner)
     parts = pl.pallas_call(
         functools.partial(rest_kernel, spacing),
         out_shape=f32(chips * 96, LANES),
-        in_specs=[VMEM] * 8,
+        in_specs=[VMEM] * 7,
         out_specs=VMEM,
         scratch_shapes=[
             pltpu.VMEM((tiles, PITCH, LANES), jnp.float32),
@@ -338,7 +376,7 @@
         compiler_params=pltpu.CompilerParams(vmem_limit_bytes=16 << 20),
         cost_estimate=cost(1 << 24, 1 << 21),
         name="rest",
-    )(state, last, behind0, behind1, edge, inner, beside, corner)
+    )(state, nearest, outer, edge, inner, beside, corner)
     slabs = lax.all_to_all(
         parts.reshape(chips, 96, LANES),
         "depth",

time: 45.6 us -> 43.7 us (0.958)
  waiting for transfers between devices: 1.56 us -> 0.01 us
  starting transfers between devices: 10.5 us -> 9.98 us
    ppermute x3 -> x2, waiting for transfers between devices: 1.56 us -> 0.01 us  [the longest x1 0.01 us: local(): lax.ppermute(outer_out, 'depth', [(2 * k + 2, 2 * k) for k in range(chips...]
    ppermute x1, starting transfers between devices: 4.65 us -> 3.48 us  [local(): beside = lax.ppermute(edge, ('depth', 'tile'), across)]
    ppermute x3 -> x2, starting transfers between devices: 3.27 us -> 3.93 us  [the longest x1 3.27 us: local(): lax.ppermute(outer_out, 'depth', [(2 * k + 2, 2 * k) for k in range(chips...]
    unnamed x2 -> x4, local copies, waits for them, and re-layouts: 1.4 us -> 1.4 us
  transfers between devices with their start and end apart: 5 -> 4, of which waited for: 1 -> 0; matrix products, arithmetic and copies ran while one was open for 0% -> 0% of each run, Pallas kernels for 10% -> 10%
where the time goes in v3:
time: 43.7 us; the launch traced here: 43.4 us
  blocking collectives  25.6 us (59%)
  starting transfers between devices  9.98 us (23%)
  Pallas kernels  6.34 us (15%)
  local copies, waits for them, and re-layouts  1.4 us (3%)
    all_to_all x1, blocking collectives, local(): lax.all_to_all(parts.reshape(chips, 96, LANES), 'depth', split_axis=0, co...  25.6 us
    pallas_call x1, Pallas kernels, local(): pl.pallas_call(functools.partial(bulk_kernel, spacing), out_shape=(f32(5,...  4.18 us
    ppermute x1, starting transfers between devices, local(): beside = lax.ppermute(edge, ('depth', 'tile'), across)  3.48 us
    ppermute x1, starting transfers between devices, local(): lax.ppermute(outer_out, 'depth', [(2 * k + 2, 2 * k) for k in range(chips...  3.27 us
    ppermute x1, starting transfers between devices, local(): partner = lax.ppermute(field, 'depth', [(i, i ^ 1) for i in range(depth)])  2.57 us
    unnamed x4, local copies, waits for them, and re-layouts  1.4 us
    pallas_call x1, Pallas kernels, local(): pl.pallas_call(functools.partial(rest_kernel, spacing), out_shape=f32(chi...  1.34 us
  transfers between devices with their start and end apart: 4, of which 0 were waited for; matrix products, arithmetic and copies ran while one was open for 0% of the time, Pallas kernels for 10%

profile of v3, /device:TPU:225, one launch (start us, length us, event | category | flops | bytes accessed | tf_op | source)
XLA Modules:
  0.0 43.4 jit_solution(16080031393540750813)
XLA Ops:
  0.0 2.6 %collective-permute-start = (f32[4,96,1024]{2,1,0:T(8,128)}, f32[4,96,1024]{2,1,0:T(8,128)S(1)}, u32[]{:S(2)}, u32[]{:S(2)}) collective-permute-start(f32[4,96,1024]{2,1,0:T(8,128)} %own.3), channel_id=1, source_target_pairs={{0,16},{16,0},{32,48},{48,32},{64,80},{80,64},{96,112},{112,96},{1... | collective-permute-start | bytes 4718600 | tf_op jit(solution)/shard_map/ppermute | solution.py:316
  2.6 0.0 copy-start
  2.6 1.4 %copy-done = f32[4,96,1024]{2,1,0:T(8,128)S(1)} copy-done((f32[4,96,1024]{2,1,0:T(8,128)S(1)}, f32[4,96,1024]{2,1,0:T(8,128)}, u32[]{:S(2)}) %copy-start) | copy-done | bytes 1572888
  4.0 0.0 copy-start.1
  4.0 3.3 %collective-permute-start.1 = (f32[1,96,1024]{2,1,0:T(8,128)S(1)}, f32[1,96,1024]{2,1,0:T(8,128)S(1)}, u32[]{:S(2)}, u32[]{:S(2)}) collective-permute-start(f32[1,96,1024]{2,1,0:T(8,128)S(1)} %outermost.1), channel_id=1, source_target_pairs={{32,0},{64,32},{96,64},{128,96},{160,128},{192,160},{224,192},{256... | collective-permute-start | bytes 1179656 | tf_op jit(solution)/shard_map/ppermute | solution.py:326
  7.3 0.0 collective-permute-done.partner
  7.3 0.0 copy-done.1
  7.3 0.1 edges.1
  7.4 3.5 %collective-permute-start.2 = (f32[64,128]{1,0:T(8,128)S(1)}, f32[64,128]{1,0:T(8,128)S(1)}, u32[]{:S(2)}, u32[]{:S(2)}) collective-permute-start(f32[64,128]{1,0:T(8,128)S(1)} %get-tuple-element.12.edge), channel_id=1, source_target_pairs={{16,1},{1,16},{17,2},{2,17},{18,3},{3,18},{19,4},{4,19},{20,5},{5,... | collective-permute-start | bytes 98312 | tf_op jit(solution)/shard_map/ppermute | solution.py:351
  10.9 0.7 %collective-permute-start.3 = (f32[8,128]{1,0:T(8,128)S(1)}, f32[8,128]{1,0:T(8,128)S(1)}, u32[]{:S(2)}, u32[]{:S(2)}) collective-permute-start(f32[8,128]{1,0:T(8,128)S(1)} %get-tuple-element.14), channel_id=1, source_target_pairs={{48,1},{49,2},{50,3},{51,4},{52,5},{53,6},{54,7},{55,8},{56,9},{57... | collective-permute-start | bytes 12296 | tf_op jit(solution)/shard_map/ppermute | solution.py:352
  11.6 4.2 %bulk.1 = (f32[5,6,64,128]{3,2,1,0:T(8,128)S(1)}, f32[8,112,128]{2,1,0:T(8,128)S(1)}) custom-call(f32[4,96,1024]{2,1,0:T(8,128)S(1)} %copy-done.1, f32[4,96,1024]{2,1,0:T(8,128)S(1)} %collective-permute-done.partner), custom_call_target="tpu_custom_call" | custom-call | flops 134217728 | bytes 4194304 | tf_op jit(solution)/shard_map/bulk/pallas_call | solution.py:354
  15.8 0.0 collective-permute-done.1.outer
  15.8 0.0 collective-permute-done.3.corner
  15.8 0.0 collective-permute-done.2.beside
  15.8 1.3 %rest.1 = f32[1536,128]{1,0:T(8,128)S(1)} custom-call(f32[5,6,64,128]{3,2,1,0:T(8,128)S(1)} %get-tuple-element.10.state, f32[8,112,128]{2,1,0:T(8,128)S(1)} %get-tuple-element.11.nearest, f32[1,96,1024]{2,1,0:T(8,128)S(1)} %collective-permute-done.1.outer, f32[64,128]{1,0:T(8,128)S(1)} %get-tuple-element.12.edge, f32[64,128]{1,0:T(8,128)S(1)} %get-tuple-element.13.inner, ...), custom_call_target="tpu_custom_call" | custom-call | flops 16777216 | bytes 2097152 | tf_op jit(solution)/shard_map/rest/pallas_call | solution.py:367
  17.1 25.6 %all_to_all.5 = f32[16,96,128]{2,1,0:T(8,128)S(1)} all-to-all(f32[16,96,128]{2,1,0:T(8,128)S(1)} %bitcast.4), channel_id=1, replica_groups={{0,32,64,96,128,160,192,224,256,288,320,352,384,416,448,480},{16,48,80,..., dimensions={0} | all-to-all | bytes 1572864 | tf_op jit(solution)/shard_map/all_to_all | solution.py:380
  42.7 0.7 %blend.1 = f32[3,4,1024]{2,1,0:T(4,128)} custom-call(f32[1536,128]{1,0:T(8,128)S(1)} %bitcast.3), custom_call_target="tpu_custom_call" | custom-call | tf_op jit(solution)/shard_map/blend/pallas_call | solution.py:388
  (1 shorter events, 0.0 us)
Async XLA Ops:
  0.0 7.3 %collective-permute-start = (f32[4,96,1024]{2,1,0:T(8,128)}, f32[4,96,1024]{2,1,0:T(8,128)S(1)}, u32[]{:S(2)}, u32[]{:S(2)}) collective-permute-start(f32[4,96,1024]{2,1,0:T(8,128)} %own.3), channel_id=1, source_target_pairs={{0,16},{16,0},{32,48},{48,32},{64,80},{80,64},{96,112},{112,96},{1... | collective-permute-start | bytes 4718600 | tf_op jit(solution)/shard_map/ppermute | solution.py:316
  2.6 1.4 %copy-start = (f32[4,96,1024]{2,1,0:T(8,128)S(1)}, f32[4,96,1024]{2,1,0:T(8,128)}, u32[]{:S(2)}) copy-start(f32[4,96,1024]{2,1,0:T(8,128)} %own.3) | copy-start | bytes 4718596
  4.0 3.3 %copy-start.1 = (f32[4,96,1024]{2,1,0:T(8,128)S(1)}, f32[4,96,1024]{2,1,0:T(8,128)}, u32[]{:S(2)}) copy-start(f32[4,96,1024]{2,1,0:T(8,128)} %own.3) | copy-start | bytes 4718596
  4.0 11.7 %collective-permute-start.1 = (f32[1,96,1024]{2,1,0:T(8,128)S(1)}, f32[1,96,1024]{2,1,0:T(8,128)S(1)}, u32[]{:S(2)}, u32[]{:S(2)}) collective-permute-start(f32[1,96,1024]{2,1,0:T(8,128)S(1)} %outermost.1), channel_id=1, source_target_pairs={{32,0},{64,32},{96,64},{128,96},{160,128},{192,160},{224,192},{256... | collective-permute-start | bytes 1179656 | tf_op jit(solution)/shard_map/ppermute | solution.py:326
  7.4 8.4 %collective-permute-start.2 = (f32[64,128]{1,0:T(8,128)S(1)}, f32[64,128]{1,0:T(8,128)S(1)}, u32[]{:S(2)}, u32[]{:S(2)}) collective-permute-start(f32[64,128]{1,0:T(8,128)S(1)} %get-tuple-element.12.edge), channel_id=1, source_target_pairs={{16,1},{1,16},{17,2},{2,17},{18,3},{3,18},{19,4},{4,19},{20,5},{5,... | collective-permute-start | bytes 98312 | tf_op jit(solution)/shard_map/ppermute | solution.py:351
  10.9 4.9 %collective-permute-start.3 = (f32[8,128]{1,0:T(8,128)S(1)}, f32[8,128]{1,0:T(8,128)S(1)}, u32[]{:S(2)}, u32[]{:S(2)}) collective-permute-start(f32[8,128]{1,0:T(8,128)S(1)} %get-tuple-element.14), channel_id=1, source_target_pairs={{48,1},{49,2},{50,3},{51,4},{52,5},{53,6},{54,7},{55,8},{56,9},{57... | collective-permute-start | bytes 12296 | tf_op jit(solution)/shard_map/ppermute | solution.py:352

commit v4 on v3

v4 whole, which is shorter than its diff:
```python
import functools
import math

import jax
import jax.numpy as jnp
from jax import lax
from jax.experimental import pallas as pl
from jax.experimental.pallas import tpu as pltpu
from jax.sharding import PartitionSpec as P


centres = (-1.2, 0.3, 1.5)
spreads = (0.25, 0.35, 0.3)
heights = (2.0, 1.0, 3.0)
floor_density = 0.05
light_cols = 0.48
light_rows = 0.6
light_depth = 0.64

LANES = 128
LOG2E = math.log2(math.e)
FIRST = 8
PITCH = 112
VMEM = pl.BlockSpec(memory_space=pltpu.VMEM)


def sample_step(spacing, state, low, high, half, above, below, slope_cols):
    run, through, total, tilt, middle = state
    run = run - spacing * LOG2E * floor_density
    for centre, spread, bump in zip(centres, spreads, heights):
        offset = half - 0.5 * centre
        run = run - jnp.exp2(
            (offset * offset) * (-4.0 * LOG2E / (spread * spread)) + math.log2(bump * spacing * LOG2E)
        )
    now = jnp.exp2(run)
    weight = through - now
    slope_rows = below - above
    slope_depth = high - low
    facing = (0.7 * light_cols) * slope_cols + (0.7 * light_rows) * slope_rows + (0.7 * light_depth) * slope_depth
    length = slope_cols * slope_cols + slope_rows * slope_rows + slope_depth * slope_depth + 1.0
    lit = weight * (0.3 + jnp.abs(facing) * lax.rsqrt(length))
    total = total + lit
    tilt = tilt + lit * jnp.tanh(2.0 * half)
    middle = middle + lit * jnp.exp2((half * half) * (-4.0 * LOG2E))
    return run, now, total, tilt, middle


def lane_masks():
    lane = lax.broadcasted_iota(jnp.int32, (8, LANES), 1)
    return lane == 0, lane == LANES - 1


def tile_slopes(half):
    leftmost, rightmost = lane_masks()
    right = [pltpu.roll(h, LANES - 1, 1) for h in half]
    left = [pltpu.roll(h, 1, 1) for h in half]
    zero = jnp.zeros_like(half[0])
    slopes = []
    for tile in range(len(half)):
        upper = jnp.where(rightmost, right[tile + 1] if tile + 1 < len(half) else zero, right[tile])
        lower = jnp.where(leftmost, left[tile - 1] if tile else zero, left[tile])
        slopes.append(upper - lower)
    return slopes


def row_slopes(half):
    leftmost, rightmost = lane_masks()
    tile = lax.broadcasted_iota(jnp.int32, (8, LANES), 0)
    right = pltpu.roll(half, LANES - 1, 1)
    left = pltpu.roll(half, 1, 1)
    upper = jnp.where(rightmost, jnp.where(tile == 7, 0.0, pltpu.roll(right, 7, 0)), right)
    lower = jnp.where(leftmost, jnp.where(tile == 0, 0.0, pltpu.roll(left, 1, 0)), left)
    return upper - lower


def core_index():
    return lax.rem(lax.axis_index("depth"), 2)


def fetch_kernel(field, own, outer, sems):
    planes, rows, width = field.shape
    copies = [pltpu.make_async_copy(field.at[pl.ds((planes - 1) * core_index(), 1)], outer, sems.at[0])]
    for tile in range(width // LANES):
        copies.append(
            pltpu.make_async_copy(
                field.at[:, :, pl.ds(tile * LANES, LANES)],
                own.at[:, tile, pl.ds(FIRST, rows), :],
                sems.at[1 + tile],
            )
        )
    for copy in copies:
        copy.start()
    for copy in copies:
        copy.wait()


def edge_kernel(own, partner, outer, sent, edge, inner):
    planes, rows, width = partner.shape
    core = core_index()

    def row(plane, tile, n):
        lanes = slice(tile * LANES, (tile + 1) * LANES)

        def mine(slot, at):
            return own[slot, tile, FIRST + at : FIRST + at + 1, :]

        def other(slot, at):
            return partner[slot, at : at + 1, lanes]

        def beyond(slot, at):
            return outer[0, at : at + 1, lanes]

        if plane == 2 * planes:
            at_core0 = at_core1 = beyond
        else:
            at_core0, at_core1 = (mine, other) if plane < planes else (other, mine)
        return jnp.where(core == 0, at_core0(plane % planes, n), at_core1(plane % planes, rows - 1 - n))

    for plane in range(2 * planes + 1):
        for tile in range(width // LANES):
            at = plane * (width // LANES) + tile
            edge[at : at + 1, :] = row(plane, tile, 0)
            inner[at : at + 1, :] = row(plane, tile, 1)
            sent[at : at + 1, :] = row(plane, tile, rows - 1)


def start_state():
    zero = jnp.zeros((8, LANES), jnp.float32)
    return zero, zero + 1.0, zero, zero, zero


def picker(buf, core):
    def picked(plane, tile, group, offset):
        return buf[plane, tile, pl.ds(FIRST + 48 * group + 3 * core + offset, 8, stride=6), :]

    return picked


def slope_pass(picked, cols, samples, groups, tiles, ends=False):
    def step(index, carry):
        group, row = index // 3, lax.rem(index, 3)
        before = [picked(samples.start, tile, group, row) for tile in range(tiles)]
        for plane in samples:
            if ends:
                half = [0.25 * a for a in before]
            else:
                after = [picked(plane + 1, tile, group, row) for tile in range(tiles)]
                half = [0.25 * (a + b) for a, b in zip(before, after)]
                before = after
            for tile, slope in enumerate(tile_slopes(half)):
                cols[plane - samples.start, index, pl.ds(tile * 8, 8), :] = slope
        return carry

    lax.fori_loop(0, 3 * groups, step, 0)


def shade_pass(spacing, picked, cols, samples, groups, tiles, load, save, ends=False):
    def step(index, carry):
        group, tile = index // tiles, lax.rem(index, tiles)
        at = [(group * 3 + row, pl.ds(tile * 8, 8)) for row in range(3)]
        low = [picked(samples.start, tile, group, offset) for offset in range(-1, 4)]
        states = [load(*at[row]) for row in range(3)]
        for plane in samples:
            if ends:
                high = [jnp.zeros_like(low[0])] * 5
                half = [0.25 * a for a in low]
            else:
                high = [picked(plane + 1, tile, group, offset) for offset in range(-1, 4)]
                half = [0.25 * (a + b) for a, b in zip(low, high)]
            for row in range(3):
                states[row] = sample_step(
                    spacing,
                    states[row],
                    low[row + 1],
                    high[row + 1],
                    half[row + 1],
                    half[row],
                    half[row + 2],
                    cols[plane - samples.start, at[row][0], at[row][1], :],
                )
            low = high
        for row in range(3):
            save(*at[row], states[row])
        return carry

    lax.fori_loop(0, groups * tiles, step, 0)


def join(first, nearer, farther):
    near_through, *near_sums = nearer
    far_through, *far_sums = farther
    on_near = jnp.where(first, 1.0, far_through)
    on_far = jnp.where(first, near_through, 1.0)
    return (near_through * far_through, *[on_near * a + on_far * b for a, b in zip(near_sums, far_sums)])


def own_kernel(spacing, own, sums, cols):
    planes, tiles = own.shape[:2]
    groups = sums.shape[1] // 3
    picked = picker(own, core_index())

    def load(block, part):
        return tuple(sums[n, block, part, :] for n in range(5))

    def save(block, part, state):
        for n, value in enumerate(state):
            sums[n, block, part, :] = value

    inside = range(planes - 1)
    slope_pass(picked, cols, inside, groups, tiles)
    shade_pass(spacing, picked, cols, inside, groups, tiles, lambda *_: start_state(), save)

    @pl.when(lax.axis_index("depth") == lax.axis_size("depth") - 1)
    def _():
        last = range(planes - 1, planes)
        slope_pass(picked, cols, last, groups, tiles, ends=True)
        shade_pass(spacing, picked, cols, last, groups, tiles, load, save, ends=True)


def partner_kernel(spacing, own, partner, own_sums, sums, nearest, buf, cols):
    planes, rows, width = partner.shape
    tiles, groups = width // LANES, rows // 48
    core = core_index()
    for tile in range(tiles):
        lanes = slice(tile * LANES, (tile + 1) * LANES)
        for plane in range(planes):
            buf[plane + 1 - core, tile, FIRST : FIRST + rows, :] = partner[plane, :, lanes]
        buf[planes * core, tile, :, :] = jnp.where(core == 0, own[planes - 1, tile], own[0, tile])
    nearest[...] = buf[planes * (1 - core)]
    picked = picker(buf, core)

    def save(block, part, state):
        nearer = tuple(own_sums[n, block, part, :] for n in range(1, 5))
        for n, value in enumerate(join(core == 0, nearer, state[1:])):
            sums[n, block, part, :] = value

    samples = range(planes)
    slope_pass(picked, cols, samples, groups, tiles)
    shade_pass(spacing, picked, cols, samples, groups, tiles, lambda *_: start_state(), save)


def finished(core, present, bulk, outer):
    outer = (jnp.where(present, outer[0], 1.0), *[jnp.where(present, value, 0.0) for value in outer[1:]])
    through, total, tilt, middle = join(core == 0, bulk, outer)
    return 0.5 * (total + tilt), middle, 0.5 * (total - tilt), through


def outer_kernel(spacing, sums, nearest, outer, edge, inner, beside, out, buf, cols):
    tiles = nearest.shape[0]
    rows = outer.shape[1]
    groups = rows // 48
    core = core_index()
    present = lax.axis_index("depth") != 1
    for tile in range(tiles):
        buf[tile, FIRST : FIRST + rows, :] = outer[0, :, tile * LANES : (tile + 1) * LANES]
    to_high = jnp.where(core == 0, 1.0, -1.0)

    def picked(ref, tile, group, offset):
        return ref[tile, pl.ds(FIRST + 48 * group + 3 * core + offset, 8, stride=6), :]

    for index in range(3 * groups):
        group, row = divmod(index, 3)
        half = [0.25 * (picked(nearest, tile, group, row) + picked(buf, tile, group, row)) for tile in range(tiles)]
        for tile, slope in enumerate(tile_slopes(half)):
            cols[index, tile * 8 : tile * 8 + 8, :] = slope

    def shade(index, carry):
        group, tile = index // tiles, lax.rem(index, tiles)
        near = [picked(nearest, tile, group, offset) for offset in range(-1, 4)]
        far = [picked(buf, tile, group, offset) for offset in range(-1, 4)]
        half = [0.25 * (a + b) for a, b in zip(near, far)]
        for row in range(3):
            sample = sample_step(
                spacing,
                start_state(),
                to_high * near[row + 1],
                to_high * far[row + 1],
                half[row + 1],
                half[row],
                half[row + 2],
                cols[group * 3 + row, pl.ds(tile * 8, 8), :],
            )
            bulk = tuple(sums[n, group * 3 + row, pl.ds(tile * 8, 8), :] for n in range(4))
            for channel, value in enumerate(finished(core, present, bulk, sample[1:])):
                out[pl.ds(group * 768 + row * 32 + channel * 8 + tile, 8, stride=96), :] = value
        return carry

    lax.fori_loop(0, groups * tiles, shade, 0)

    planes = edge.shape[0] // 8 - 1

    def plane_rows(plane):
        at = slice(plane * 8, plane * 8 + 8)
        return edge[at, :], inner[at, :], beside[at, :]

    def line_step(line, low, high):
        half, within, beyond = [0.25 * (a + b) for a, b in zip(low, high)]
        above = jnp.where(core == 0, beyond, within)
        below = jnp.where(core == 0, within, beyond)
        return sample_step(spacing, line, low[0], high[0], half, above, below, row_slopes(half))

    line = start_state()
    for plane in range(planes - 1):
        line = line_step(line, plane_rows(plane), plane_rows(plane + 1))
    zero = jnp.zeros((8, LANES), jnp.float32)
    ended = line_step(line, plane_rows(planes - 1), (zero, zero, zero))
    at_end = lax.axis_index("depth") == lax.axis_size("depth") - 1
    line = tuple(jnp.where(at_end, a, b) for a, b in zip(ended, line))
    far = plane_rows(planes)
    near = [jnp.where(core == 0, a, b) for a, b in zip(plane_rows(planes - 1), plane_rows(0))]
    low = [jnp.where(core == 0, a, b) for a, b in zip(near, far)]
    high = [jnp.where(core == 0, b, a) for a, b in zip(near, far)]
    sample = line_step(start_state(), low, high)
    place = core * (out.shape[0] - 32)
    for channel, value in enumerate(finished(core, present, line[1:], sample[1:])):
        out[pl.ds(pl.multiple_of(place + channel * 8, 8), 8), :] = value


def blend_kernel(slabs, out):
    count = slabs.shape[0] // 96
    for row in range(3):
        through = jnp.ones((8, LANES), jnp.float32)
        colour = [jnp.zeros((8, LANES), jnp.float32)] * 3
        for slab in range(count):
            base = slab * 96 + row * 32
            for channel in range(3):
                colour[channel] = colour[channel] + through * slabs[base + channel * 8 : base + channel * 8 + 8, :]
            through = through * slabs[base + 24 : base + 32, :]
        for channel, value in enumerate((*colour, 1.0 - through)):
            for tile in range(8):
                out[row, channel : channel + 1, tile * LANES : (tile + 1) * LANES] = value[tile : tile + 1, :]


def f32(*shape):
    return jax.ShapeDtypeStruct(shape, jnp.float32)


def cost(flops, size):
    return pl.CostEstimate(flops=flops, bytes_accessed=size, transcendentals=0)


def composited(field):
    planes, rows, width = field.shape
    depth = lax.axis_size("depth")
    strips = lax.axis_size("tile")
    chips = depth // 2
    tiles = width // LANES
    spacing = 3.0 / (planes * depth)

    own, outer_out = pl.pallas_call(
        fetch_kernel,
        out_shape=(f32(planes, tiles, PITCH, LANES), f32(1, rows, width)),
        in_specs=[pl.BlockSpec(memory_space=pltpu.HBM)],
        out_specs=(VMEM, VMEM),
        scratch_shapes=[pltpu.SemaphoreType.DMA((1 + tiles,))],
        compiler_params=pltpu.CompilerParams(vmem_limit_bytes=4 << 20),
        cost_estimate=cost(1 << 10, 1 << 22),
        name="fetch",
    )(field)
    outer = lax.ppermute(
        outer_out,
        "depth",
        [(2 * k + 2, 2 * k) for k in range(chips - 1)] + [(2 * k + 1, 2 * k + 3) for k in range(chips - 1)],
    )
    partner = lax.ppermute(field, "depth", [(i, i ^ 1) for i in range(depth)])

    lines = (2 * planes + 1) * tiles
    sent, edge, inner = pl.pallas_call(
        edge_kernel,
        out_shape=(f32(lines, LANES), f32(lines, LANES), f32(lines, LANES)),
        in_specs=[VMEM, VMEM, VMEM],
        out_specs=(VMEM, VMEM, VMEM),
        compiler_params=pltpu.CompilerParams(vmem_limit_bytes=4 << 20),
        cost_estimate=cost(1 << 20, 1 << 19),
        name="edges",
    )(own, partner, outer)
    place = lambda d, s: d * strips + s
    beside = lax.ppermute(
        sent,
        ("depth", "tile"),
        [(place(2 * k, t), place(2 * k, t + 1)) for k in range(chips) for t in range(strips - 1)]
        + [(place(2 * k + 1, t + 1), place(2 * k + 1, t)) for k in range(chips) for t in range(strips - 1)],
    )

    blocks = rows // 16
    own_sums = pl.pallas_call(
        functools.partial(own_kernel, spacing),
        out_shape=f32(5, blocks, tiles * 8, LANES),
        in_specs=[VMEM],
        out_specs=VMEM,
        scratch_shapes=[
                pltpu.VMEM((planes - 1, blocks, tiles * 8, LANES), jnp.float32),
        ],
        compiler_params=pltpu.CompilerParams(vmem_limit_bytes=12 << 20),
        cost_estimate=cost(1 << 26, 1 << 21),
        name="own",
    )(own)
    sums, nearest = pl.pallas_call(
        functools.partial(partner_kernel, spacing),
        out_shape=(f32(4, blocks, tiles * 8, LANES), f32(tiles, PITCH, LANES)),
        in_specs=[VMEM] * 3,
        out_specs=(VMEM, VMEM),
        scratch_shapes=[
            pltpu.VMEM((planes + 1, tiles, PITCH, LANES), jnp.float32),
            pltpu.VMEM((planes, blocks, tiles * 8, LANES), jnp.float32),
        ],
        compiler_params=pltpu.CompilerParams(vmem_limit_bytes=12 << 20),
        cost_estimate=cost(1 << 26, 1 << 21),
        name="partner",
    )(own, partner, own_sums)
    parts = pl.pallas_call(
        functools.partial(outer_kernel, spacing),
        out_shape=f32(chips * 96, LANES),
        in_specs=[VMEM] * 6,
        out_specs=VMEM,
        scratch_shapes=[
            pltpu.VMEM((tiles, PITCH, LANES), jnp.float32),
            pltpu.VMEM((rows // 16, tiles * 8, LANES), jnp.float32),
        ],
        compiler_params=pltpu.CompilerParams(vmem_limit_bytes=16 << 20),
        cost_estimate=cost(1 << 24, 1 << 21),
        name="outer",
    )(sums, nearest, outer, edge, inner, beside)
    slabs = lax.all_to_all(
        parts.reshape(chips, 96, LANES),
        "depth",
        split_axis=0,
        concat_axis=0,
        tiled=True,
        axis_index_groups=[[2 * k + c for k in range(chips)] for c in range(2)],
    )
    image = pl.pallas_call(
        blend_kernel,
        out_shape=f32(3, 4, width),
        in_specs=[VMEM],
        out_specs=VMEM,
        compiler_params=pltpu.CompilerParams(vmem_limit_bytes=8 << 20),
        name="blend",
    )(slabs.reshape(chips * 96, LANES))
    return jnp.transpose(image, (1, 0, 2))


def solution(mesh):
    return jax.shard_map(
        composited,
        mesh=mesh,
        in_specs=(P("depth", "tile", None),),
        out_specs=P(None, ("tile", "depth"), None),
        check_vma=False,
    )
```

time: 43.7 us -> 46 us (1.053)
  the two profiles are of different devices: /device:TPU:225 before, /device:TPU:384 now
where the time goes in v4:
time: 46 us; the launch traced here: 45.8 us
  blocking collectives  22.4 us (49%)
  waiting for transfers between devices  8.38 us (18%)
  Pallas kernels  7.48 us (16%)
  starting transfers between devices  6.13 us (13%)
  local copies, waits for them, and re-layouts  1.4 us (3%)
    all_to_all x1, blocking collectives, composited(): lax.all_to_all(parts.reshape(chips, 96, LANES), 'depth', split_axis=0, co...  22.4 us
    ppermute x1, waiting for transfers between devices, composited(): lax.ppermute(outer_out, 'depth', [(2 * k + 2, 2 * k) for k in range(chips...  8.37 us
    ppermute x1, starting transfers between devices, composited(): lax.ppermute(sent, ('depth', 'tile'), [(place(2 * k, t), place(2 * k, t +...  2.93 us
    pallas_call x1, Pallas kernels, composited(): pl.pallas_call(functools.partial(partner_kernel, spacing), out_shape=(f32...  2.75 us
    pallas_call x1, Pallas kernels, composited(): pl.pallas_call(functools.partial(own_kernel, spacing), out_shape=f32(5, b...  2.05 us
    ppermute x1, starting transfers between devices, composited(): partner = lax.ppermute(field, 'depth', [(i, i ^ 1) for i in range(depth)])  1.91 us
    pallas_call x1, Pallas kernels, composited(): pl.pallas_call(functools.partial(outer_kernel, spacing), out_shape=f32(ch...  1.4 us
    unnamed x2, local copies, waits for them, and re-layouts  1.4 us
  transfers between devices with their start and end apart: 3, of which 1 were waited for; matrix products, arithmetic and copies ran while one was open for 0% of the time, Pallas kernels for 12%

profile of v4, /device:TPU:384, one launch (start us, length us, event | category | flops | bytes accessed | tf_op | source)
XLA Modules:
  0.0 45.8 jit_solution(15191280802591539306)
XLA Ops:
  0.0 1.9 %collective-permute-start = (f32[4,96,1024]{2,1,0:T(8,128)}, f32[4,96,1024]{2,1,0:T(8,128)S(1)}, u32[]{:S(2)}, u32[]{:S(2)}) collective-permute-start(f32[4,96,1024]{2,1,0:T(8,128)} %field.1), channel_id=1, source_target_pairs={{0,16},{16,0},{32,48},{48,32},{64,80},{80,64},{96,112},{112,96},{1... | collective-permute-start | bytes 4718600 | tf_op jit(solution)/shard_map/ppermute | solution.py:365
  1.9 0.0 copy-start
  1.9 1.4 %copy-done = f32[4,96,1024]{2,1,0:T(8,128)S(1)} copy-done((f32[4,96,1024]{2,1,0:T(8,128)S(1)}, f32[4,96,1024]{2,1,0:T(8,128)}, u32[]{:S(2)}) %copy-start) | copy-done | bytes 1572888
  3.3 0.5 %fetch.1 = (f32[4,8,112,128]{3,2,1,0:T(8,128)S(1)}, f32[1,96,1024]{2,1,0:T(8,128)S(1)}) custom-call(f32[4,96,1024]{2,1,0:T(8,128)S(1)} %copy-done), custom_call_target="tpu_custom_call" | custom-call | flops 1024 | bytes 4194304 | tf_op jit(solution)/shard_map/fetch/pallas_call | solution.py:350
  3.8 1.3 %collective-permute-start.1 = (f32[1,96,1024]{2,1,0:T(8,128)S(1)}, f32[1,96,1024]{2,1,0:T(8,128)S(1)}, u32[]{:S(2)}, u32[]{:S(2)}) collective-permute-start(f32[1,96,1024]{2,1,0:T(8,128)S(1)} %get-tuple-element.15), channel_id=1, source_target_pairs={{32,0},{64,32},{96,64},{128,96},{160,128},{192,160},{224,192},{256... | collective-permute-start | bytes 1179656 | tf_op jit(solution)/shard_map/ppermute | solution.py:360
  5.1 8.4 %collective-permute-done.1.outer = f32[1,96,1024]{2,1,0:T(8,128)S(1)} collective-permute-done((f32[1,96,1024]{2,1,0:T(8,128)S(1)}, f32[1,96,1024]{2,1,0:T(8,128)S(1)}, u32[]{:S(2)}, u32[]{:S(2)}) %collective-permute-start.1) | collective-permute-done | bytes 393248 | tf_op jit(solution)/shard_map/ppermute | solution.py:360
  13.5 0.0 collective-permute-done.partner
  13.5 0.1 edges.1
  13.6 2.9 %collective-permute-start.2 = (f32[72,128]{1,0:T(8,128)S(1)}, f32[72,128]{1,0:T(8,128)S(1)}, u32[]{:S(2)}, u32[]{:S(2)}) collective-permute-start(f32[72,128]{1,0:T(8,128)S(1)} %get-tuple-element.18), channel_id=1, source_target_pairs={{0,1},{1,2},{2,3},{3,4},{4,5},{5,6},{6,7},{7,8},{8,9},{9,10},{10,1... | collective-permute-start | bytes 110600 | tf_op jit(solution)/shard_map/ppermute | solution.py:378
  16.5 2.1 %own.1.own_sums = f32[5,6,64,128]{3,2,1,0:T(8,128)S(1)} custom-call(f32[4,8,112,128]{3,2,1,0:T(8,128)S(1)} %get-tuple-element.12.own), custom_call_target="tpu_custom_call" | custom-call | flops 67108864 | bytes 2097152 | tf_op jit(solution)/shard_map/own/pallas_call | solution.py:386
  18.6 2.7 %partner.1 = (f32[4,6,64,128]{3,2,1,0:T(8,128)S(1)}, f32[8,112,128]{2,1,0:T(8,128)S(1)}) custom-call(f32[4,8,112,128]{3,2,1,0:T(8,128)S(1)} %get-tuple-element.12.own, f32[4,96,1024]{2,1,0:T(8,128)S(1)} %collective-permute-done.partner, f32[5,6,64,128]{3,2,1,0:T(8,128)S(1)} %own.1.own_sums), custom_call_target="tpu_custom_call" | custom-call | flops 67108864 | bytes 2097152 | tf_op jit(solution)/shard_map/partner/pallas_call | solution.py:398
  21.4 0.0 collective-permute-done.2.beside
  21.4 1.4 %outer.1 = f32[1536,128]{1,0:T(8,128)S(1)} custom-call(f32[4,6,64,128]{3,2,1,0:T(8,128)S(1)} %get-tuple-element.13.sums, f32[8,112,128]{2,1,0:T(8,128)S(1)} %get-tuple-element.14.nearest, f32[1,96,1024]{2,1,0:T(8,128)S(1)} %collective-permute-done.1.outer, f32[72,128]{1,0:T(8,128)S(1)} %get-tuple-element.16.edge, f32[72,128]{1,0:T(8,128)S(1)} %get-tuple-element.17.inner, ...), custom_call_target="tpu_custom_call" | custom-call | flops 16777216 | bytes 2097152 | tf_op jit(solution)/shard_map/outer/pallas_call | solution.py:411
  22.8 22.4 %all_to_all.5 = f32[16,96,128]{2,1,0:T(8,128)S(1)} all-to-all(f32[16,96,128]{2,1,0:T(8,128)S(1)} %bitcast.3), channel_id=1, replica_groups={{0,32,64,96,128,160,192,224,256,288,320,352,384,416,448,480},{16,48,80,..., dimensions={0} | all-to-all | bytes 1572864 | tf_op jit(solution)/shard_map/all_to_all | solution.py:424
  45.1 0.7 %blend.1 = f32[3,4,1024]{2,1,0:T(4,128)} custom-call(f32[1536,128]{1,0:T(8,128)S(1)} %bitcast.4), custom_call_target="tpu_custom_call" | custom-call | tf_op jit(solution)/shard_map/blend/pallas_call | solution.py:432
Async XLA Ops:
  0.0 13.5 %collective-permute-start = (f32[4,96,1024]{2,1,0:T(8,128)}, f32[4,96,1024]{2,1,0:T(8,128)S(1)}, u32[]{:S(2)}, u32[]{:S(2)}) collective-permute-start(f32[4,96,1024]{2,1,0:T(8,128)} %field.1), channel_id=1, source_target_pairs={{0,16},{16,0},{32,48},{48,32},{64,80},{80,64},{96,112},{112,96},{1... | collective-permute-start | bytes 4718600 | tf_op jit(solution)/shard_map/ppermute | solution.py:365
  1.9 1.4 %copy-start = (f32[4,96,1024]{2,1,0:T(8,128)S(1)}, f32[4,96,1024]{2,1,0:T(8,128)}, u32[]{:S(2)}) copy-start(f32[4,96,1024]{2,1,0:T(8,128)} %field.1) | copy-start | bytes 4718596
  3.8 9.7 %collective-permute-start.1 = (f32[1,96,1024]{2,1,0:T(8,128)S(1)}, f32[1,96,1024]{2,1,0:T(8,128)S(1)}, u32[]{:S(2)}, u32[]{:S(2)}) collective-permute-start(f32[1,96,1024]{2,1,0:T(8,128)S(1)} %get-tuple-element.15), channel_id=1, source_target_pairs={{32,0},{64,32},{96,64},{128,96},{160,128},{192,160},{224,192},{256... | collective-permute-start | bytes 1179656 | tf_op jit(solution)/shard_map/ppermute | solution.py:360
  13.6 7.8 %collective-permute-start.2 = (f32[72,128]{1,0:T(8,128)S(1)}, f32[72,128]{1,0:T(8,128)S(1)}, u32[]{:S(2)}, u32[]{:S(2)}) collective-permute-start(f32[72,128]{1,0:T(8,128)S(1)} %get-tuple-element.18), channel_id=1, source_target_pairs={{0,1},{1,2},{2,3},{3,4},{4,5},{5,6},{6,7},{7,8},{8,9},{9,10},{10,1... | collective-permute-start | bytes 110600 | tf_op jit(solution)/shard_map/ppermute | solution.py:378

commit v5 on v4

v5 whole, which is shorter than its diff:
```python
import functools
import math

import jax
import jax.numpy as jnp
from jax import lax
from jax.experimental import pallas as pl
from jax.experimental.pallas import tpu as pltpu
from jax.sharding import PartitionSpec as P


centres = (-1.2, 0.3, 1.5)
spreads = (0.25, 0.35, 0.3)
heights = (2.0, 1.0, 3.0)
floor_density = 0.05
light_cols = 0.48
light_rows = 0.6
light_depth = 0.64

LANES = 128
LOG2E = math.log2(math.e)
FIRST = 8
PITCH = 112
VMEM = pl.BlockSpec(memory_space=pltpu.VMEM)


def sample_step(spacing, state, low, high, half, above, below, slope_cols):
    run, through, total, tilt, middle = state
    run = run - spacing * LOG2E * floor_density
    for centre, spread, bump in zip(centres, spreads, heights):
        offset = half - 0.5 * centre
        run = run - jnp.exp2(
            (offset * offset) * (-4.0 * LOG2E / (spread * spread)) + math.log2(bump * spacing * LOG2E)
        )
    now = jnp.exp2(run)
    weight = through - now
    slope_rows = below - above
    slope_depth = high - low
    facing = (0.7 * light_cols) * slope_cols + (0.7 * light_rows) * slope_rows + (0.7 * light_depth) * slope_depth
    length = slope_cols * slope_cols + slope_rows * slope_rows + slope_depth * slope_depth + 1.0
    lit = weight * (0.3 + jnp.abs(facing) * lax.rsqrt(length))
    total = total + lit
    tilt = tilt + lit * jnp.tanh(2.0 * half)
    middle = middle + lit * jnp.exp2((half * half) * (-4.0 * LOG2E))
    return run, now, total, tilt, middle


def lane_masks():
    lane = lax.broadcasted_iota(jnp.int32, (8, LANES), 1)
    return lane == 0, lane == LANES - 1


def row_slopes(half):
    leftmost, rightmost = lane_masks()
    tile = lax.broadcasted_iota(jnp.int32, (8, LANES), 0)
    right = pltpu.roll(half, LANES - 1, 1)
    left = pltpu.roll(half, 1, 1)
    upper = jnp.where(rightmost, jnp.where(tile == 7, 0.0, pltpu.roll(right, 7, 0)), right)
    lower = jnp.where(leftmost, jnp.where(tile == 0, 0.0, pltpu.roll(left, 1, 0)), left)
    return upper - lower


def core_index():
    return lax.rem(lax.axis_index("depth"), 2)


def fetch_kernel(field, outer, sem):
    copy = pltpu.make_async_copy(field.at[pl.ds((field.shape[0] - 1) * core_index(), 1)], outer, sem)
    copy.start()
    copy.wait()


def edge_kernel(own, partner, outer, sent, edge, inner):
    planes, rows, width = partner.shape
    core = core_index()

    def row(plane, tile, n):
        lanes = slice(tile * LANES, (tile + 1) * LANES)

        def mine(slot, at):
            return own[slot, tile, FIRST + at : FIRST + at + 1, :]

        def other(slot, at):
            return partner[slot, at : at + 1, lanes]

        def beyond(slot, at):
            return outer[0, at : at + 1, lanes]

        if plane == 2 * planes:
            at_core0 = at_core1 = beyond
        else:
            at_core0, at_core1 = (mine, other) if plane < planes else (other, mine)
        return jnp.where(core == 0, at_core0(plane % planes, n), at_core1(plane % planes, rows - 1 - n))

    for plane in range(2 * planes + 1):
        for tile in range(width // LANES):
            at = plane * (width // LANES) + tile
            edge[at : at + 1, :] = row(plane, tile, 0)
            inner[at : at + 1, :] = row(plane, tile, 1)
            sent[at : at + 1, :] = row(plane, tile, rows - 1)


def start_state():
    zero = jnp.zeros((8, LANES), jnp.float32)
    return zero, zero + 1.0, zero, zero, zero


def picker(buf, core):
    def picked(plane, tile, group, offset):
        return buf[plane, tile, pl.ds(FIRST + 48 * group + 3 * core + offset, 8, stride=6), :]

    return picked


def plane_differences(picked, plane, tile, tiles, group, rows):
    leftmost, rightmost = lane_masks()
    left, right = jnp.where(tile == 0, tiles, tile - 1), tile + 1
    return [
        pltpu.roll(jnp.where(leftmost, picked(plane, right, group, n), row), LANES - 1, 1)
        - pltpu.roll(jnp.where(rightmost, picked(plane, left, group, n), row), 1, 1)
        for n, row in enumerate(rows)
    ]


def shade_tile(spacing, picked, samples, tile, tiles, group, last=False):
    low = [picked(samples.start, tile, group, offset) for offset in range(-1, 4)]
    low_cols = plane_differences(picked, samples.start, tile, tiles, group, low[1:4])
    states = [start_state()] * 3
    for plane in samples:
        if last:
            high, high_cols = [jnp.zeros_like(low[0])] * 5, [jnp.zeros_like(low[0])] * 3
        else:
            high = [picked(plane + 1, tile, group, offset) for offset in range(-1, 4)]
            high_cols = plane_differences(picked, plane + 1, tile, tiles, group, high[1:4])
        half = [0.25 * (a + b) for a, b in zip(low, high)]
        for row in range(3):
            states[row] = sample_step(
                spacing,
                states[row],
                low[row + 1],
                high[row + 1],
                half[row + 1],
                half[row],
                half[row + 2],
                0.25 * (low_cols[row] + high_cols[row]),
            )
        low, low_cols = high, high_cols
    return states


def join(first, nearer, farther):
    near_through, *near_sums = nearer
    far_through, *far_sums = farther
    on_near = jnp.where(first, 1.0, far_through)
    on_far = jnp.where(first, near_through, 1.0)
    return (near_through * far_through, *[on_near * a + on_far * b for a, b in zip(near_sums, far_sums)])


def own_kernel(spacing, field, own, sums, sems):
    planes, rows, width = field.shape
    tiles = width // LANES
    copies = [
        pltpu.make_async_copy(
            field.at[:, :, pl.ds(tile * LANES, LANES)], own.at[:, tile, pl.ds(FIRST, rows), :], sems.at[tile]
        )
        for tile in range(tiles)
    ]
    for copy in copies:
        copy.start()
    own[:, tiles, :, :] = jnp.zeros((planes, PITCH, LANES), jnp.float32)
    for copy in copies:
        copy.wait()
    picked = picker(own, core_index())

    def step(index, carry):
        group, tile = index // tiles, lax.rem(index, tiles)
        for row, state in enumerate(shade_tile(spacing, picked, range(planes - 1), tile, tiles, group)):
            for n, value in enumerate(state[1:]):
                sums[n, group * 3 + row, pl.ds(tile * 8, 8), :] = value
        return carry

    lax.fori_loop(0, sums.shape[1] // 3 * tiles, step, 0)


def partner_kernel(spacing, group, own, partner, own_sums, sums, buf):
    planes, _, width = partner.shape
    tiles = width // LANES
    core = core_index()
    first = 40 * group
    padded = slice(FIRST + first, FIRST + first + 56)
    for tile in range(tiles):
        for plane in range(planes):
            lanes = slice(tile * LANES, (tile + 1) * LANES)
            buf[plane + 1 - core, tile, padded, :] = partner[plane, first : first + 56, lanes]
        buf[planes * core, tile, :, :] = jnp.where(core == 0, own[planes - 1, tile], own[0, tile])
    buf[:, tiles, :, :] = jnp.zeros((planes + 1, PITCH, LANES), jnp.float32)
    picked = picker(buf, core)

    def step(tile, carry):
        part = pl.ds(tile * 8, 8)
        for row, state in enumerate(shade_tile(spacing, picked, range(planes), tile, tiles, group)):
            nearer = tuple(own_sums[n, group * 3 + row, part, :] for n in range(4))
            for n, value in enumerate(join(core == 0, nearer, state[1:])):
                sums[n, row, part, :] = value
        return carry

    lax.fori_loop(0, tiles, step, 0)

    @pl.when(lax.axis_index("depth") == lax.axis_size("depth") - 2)
    def _():
        def last_step(tile, carry):
            part = pl.ds(tile * 8, 8)
            last = range(planes, planes + 1)
            for row, state in enumerate(shade_tile(spacing, picked, last, tile, tiles, group, last=True)):
                nearer = tuple(sums[n, row, part, :] for n in range(4))
                for n, value in enumerate(join(True, nearer, state[1:])):
                    sums[n, row, part, :] = value
            return carry

        lax.fori_loop(0, tiles, last_step, 0)


def finished(core, present, bulk, outer):
    outer = (jnp.where(present, outer[0], 1.0), *[jnp.where(present, value, 0.0) for value in outer[1:]])
    through, total, tilt, middle = join(core == 1, bulk, outer)
    return 0.5 * (total + tilt), middle, 0.5 * (total - tilt), through


def outer_kernel(spacing, sums0, sums1, own, outer, out, buf):
    slots, tiles = own.shape[0], own.shape[1] - 1
    rows = outer.shape[1]
    core = core_index()
    present = lax.axis_index("depth") != 0
    for tile in range(tiles):
        buf[0, tile, FIRST : FIRST + rows, :] = outer[0, :, tile * LANES : (tile + 1) * LANES]
    buf[:, tiles, :, :] = jnp.zeros((1, PITCH, LANES), jnp.float32)
    to_high = jnp.where(core == 0, -1.0, 1.0)
    near_picked, far_picked = picker(own, core), picker(buf, core)
    nearest = (slots - 1) * core

    def shade(tile, carry):
        part = pl.ds(tile * 8, 8)
        for group, sums in enumerate((sums0, sums1)):
            near = [near_picked(nearest, tile, group, offset) for offset in range(-1, 4)]
            far = [far_picked(0, tile, group, offset) for offset in range(-1, 4)]
            near_cols = plane_differences(near_picked, nearest, tile, tiles, group, near[1:4])
            far_cols = plane_differences(far_picked, 0, tile, tiles, group, far[1:4])
            half = [0.25 * (a + b) for a, b in zip(near, far)]
            for row in range(3):
                sample = sample_step(
                    spacing,
                    start_state(),
                    to_high * near[row + 1],
                    to_high * far[row + 1],
                    half[row + 1],
                    half[row],
                    half[row + 2],
                    0.25 * (near_cols[row] + far_cols[row]),
                )
                bulk = tuple(sums[n, row, part, :] for n in range(4))
                for channel, value in enumerate(finished(core, present, bulk, sample[1:])):
                    out[pl.ds(group * 768 + row * 32 + channel * 8 + tile, 8, stride=96), :] = value
        return carry

    lax.fori_loop(0, tiles, shade, 0)


def line_kernel(spacing, main, edge, inner, beside, out, strip, sem):
    del main
    core = core_index()
    present = lax.axis_index("depth") != 0
    planes = edge.shape[0] // 8 - 1

    def plane_rows(plane):
        at = slice(plane * 8, plane * 8 + 8)
        return edge[at, :], inner[at, :], beside[at, :]

    def line_step(line, low, high):
        half, within, beyond = [0.25 * (a + b) for a, b in zip(low, high)]
        above = jnp.where(core == 0, beyond, within)
        below = jnp.where(core == 0, within, beyond)
        return sample_step(spacing, line, low[0], high[0], half, above, below, row_slopes(half))

    line = start_state()
    for plane in range(planes - 1):
        line = line_step(line, plane_rows(plane), plane_rows(plane + 1))
    zero = jnp.zeros((8, LANES), jnp.float32)
    ended = line_step(line, plane_rows(planes - 1), (zero, zero, zero))
    at_end = lax.axis_index("depth") == lax.axis_size("depth") - 2
    line = tuple(jnp.where(at_end, a, b) for a, b in zip(ended, line))
    far = plane_rows(planes)
    near = [jnp.where(core == 0, a, b) for a, b in zip(plane_rows(0), plane_rows(planes - 1))]
    low = [jnp.where(core == 0, b, a) for a, b in zip(near, far)]
    high = [jnp.where(core == 0, a, b) for a, b in zip(near, far)]
    sample = line_step(start_state(), low, high)
    for channel, value in enumerate(finished(core, present, line[1:], sample[1:])):
        strip[channel * 8 : channel * 8 + 8, :] = value
    place = pl.multiple_of(core * (out.shape[0] - 32), 8)
    copy = pltpu.make_async_copy(strip, out.at[pl.ds(place, 32)], sem)
    copy.start()
    copy.wait()


def blend_kernel(slabs, out):
    count = slabs.shape[0] // 96
    for row in range(3):
        through = jnp.ones((8, LANES), jnp.float32)
        colour = [jnp.zeros((8, LANES), jnp.float32)] * 3
        for slab in range(count):
            base = slab * 96 + row * 32
            for channel in range(3):
                colour[channel] = colour[channel] + through * slabs[base + channel * 8 : base + channel * 8 + 8, :]
            through = through * slabs[base + 24 : base + 32, :]
        for channel, value in enumerate((*colour, 1.0 - through)):
            for tile in range(8):
                out[row, channel : channel + 1, tile * LANES : (tile + 1) * LANES] = value[tile : tile + 1, :]


def f32(*shape):
    return jax.ShapeDtypeStruct(shape, jnp.float32)


def cost(flops, size):
    return pl.CostEstimate(flops=flops, bytes_accessed=size, transcendentals=0)


def composited(field):
    planes, rows, width = field.shape
    depth = lax.axis_size("depth")
    strips = lax.axis_size("tile")
    chips = depth // 2
    tiles = width // LANES
    spacing = 3.0 / (planes * depth)

    outer_out = pl.pallas_call(
        fetch_kernel,
        out_shape=f32(1, rows, width),
        in_specs=[pl.BlockSpec(memory_space=pltpu.HBM)],
        out_specs=VMEM,
        scratch_shapes=[pltpu.SemaphoreType.DMA],
        compiler_params=pltpu.CompilerParams(vmem_limit_bytes=4 << 20),
        cost_estimate=cost(1 << 10, 1 << 20),
        name="fetch",
    )(field)
    outer = lax.ppermute(
        outer_out,
        "depth",
        [(2 * k + 1, 2 * k + 2) for k in range(chips - 1)] + [(2 * k + 2, 2 * k + 1) for k in range(chips - 1)],
    )
    partner = lax.ppermute(field, "depth", [(i, i ^ 1) for i in range(depth)])

    own, own_sums = pl.pallas_call(
        functools.partial(own_kernel, spacing),
        out_shape=(f32(planes, tiles + 1, PITCH, LANES), f32(4, rows // 16, tiles * 8, LANES)),
        in_specs=[pl.BlockSpec(memory_space=pltpu.HBM)],
        out_specs=(VMEM, VMEM),
        scratch_shapes=[pltpu.SemaphoreType.DMA((tiles,))],
        compiler_params=pltpu.CompilerParams(vmem_limit_bytes=12 << 20),
        cost_estimate=cost(1 << 26, 1 << 21),
        name="own",
    )(field)

    lines = (2 * planes + 1) * tiles
    sent, edge, inner = pl.pallas_call(
        edge_kernel,
        out_shape=(f32(lines, LANES), f32(lines, LANES), f32(lines, LANES)),
        in_specs=[VMEM, VMEM, VMEM],
        out_specs=(VMEM, VMEM, VMEM),
        compiler_params=pltpu.CompilerParams(vmem_limit_bytes=4 << 20),
        cost_estimate=cost(1 << 20, 1 << 19),
        name="edges",
    )(own, partner, outer)
    place = lambda d, s: d * strips + s
    beside = lax.ppermute(
        sent,
        ("depth", "tile"),
        [(place(2 * k, t), place(2 * k, t + 1)) for k in range(chips) for t in range(strips - 1)]
        + [(place(2 * k + 1, t + 1), place(2 * k + 1, t)) for k in range(chips) for t in range(strips - 1)],
    )

    sums = []
    for group in range(2):
        sums.append(
            pl.pallas_call(
                functools.partial(partner_kernel, spacing, group),
                out_shape=f32(4, 3, tiles * 8, LANES),
                in_specs=[VMEM] * 3,
                out_specs=VMEM,
                scratch_shapes=[pltpu.VMEM((planes + 1, tiles + 1, PITCH, LANES), jnp.float32)],
                compiler_params=pltpu.CompilerParams(vmem_limit_bytes=12 << 20),
                cost_estimate=cost(1 << 25, 1 << 20),
            )(own, partner, own_sums)
        )
    most = pl.pallas_call(
        functools.partial(outer_kernel, spacing),
        out_shape=f32(chips * 96, LANES),
        in_specs=[VMEM] * 4,
        out_specs=VMEM,
        scratch_shapes=[pltpu.VMEM((1, tiles + 1, PITCH, LANES), jnp.float32)],
        compiler_params=pltpu.CompilerParams(vmem_limit_bytes=12 << 20),
        cost_estimate=cost(1 << 24, 1 << 21),
        name="outer",
    )(*sums, own, outer)
    parts = pl.pallas_call(
        functools.partial(line_kernel, spacing),
        out_shape=f32(chips * 96, LANES),
        in_specs=[pl.BlockSpec(memory_space=pl.ANY)] + [VMEM] * 3,
        out_specs=pl.BlockSpec(memory_space=pl.ANY),
        input_output_aliases={0: 0},
        scratch_shapes=[pltpu.VMEM((32, LANES), jnp.float32), pltpu.SemaphoreType.DMA],
        compiler_params=pltpu.CompilerParams(vmem_limit_bytes=4 << 20),
        cost_estimate=cost(1 << 20, 1 << 18),
        name="line",
    )(most, edge, inner, beside)
    slabs = lax.all_to_all(
        parts.reshape(chips, 96, LANES),
        "depth",
        split_axis=0,
        concat_axis=0,
        tiled=True,
        axis_index_groups=[[2 * k + c for k in range(chips)] for c in range(2)],
    )
    image = pl.pallas_call(
        blend_kernel,
        out_shape=f32(3, 4, width),
        in_specs=[VMEM],
        out_specs=VMEM,
        compiler_params=pltpu.CompilerParams(vmem_limit_bytes=8 << 20),
        name="blend",
    )(slabs.reshape(chips * 96, LANES))
    return jnp.transpose(image, (1, 0, 2))


def solution(mesh):
    return jax.shard_map(
        composited,
        mesh=mesh,
        in_specs=(P("depth", "tile", None),),
        out_specs=P(None, ("tile", "depth"), None),
        check_vma=False,
    )
```

time: 46 us -> 44.1 us (0.959)
  the two profiles are of different devices: /device:TPU:384 before, /device:TPU:385 now
where the time goes in v5:
time: 44.1 us; the launch traced here: 43.9 us
  blocking collectives  22 us (50%)
  starting transfers between devices  9.57 us (22%)
  Pallas kernels  6.98 us (16%)
  waiting for transfers between devices  3.8 us (9%)
  local copies, waits for them, and re-layouts  1.4 us (3%)
    all_to_all x1, blocking collectives, composited(): lax.all_to_all(parts.reshape(chips, 96, LANES), 'depth', split_axis=0, co...  22 us
    ppermute x1, starting transfers between devices, composited(): lax.ppermute(sent, ('depth', 'tile'), [(place(2 * k, t), place(2 * k, t +...  3.85 us
    ppermute x1, waiting for transfers between devices, composited(): lax.ppermute(outer_out, 'depth', [(2 * k + 1, 2 * k + 2) for k in range(c...  3.79 us
    ppermute x1, starting transfers between devices, composited(): lax.ppermute(outer_out, 'depth', [(2 * k + 1, 2 * k + 2) for k in range(c...  3.15 us
    ppermute x1, starting transfers between devices, composited(): partner = lax.ppermute(field, 'depth', [(i, i ^ 1) for i in range(depth)])  2.57 us
    pallas_call x2, Pallas kernels, composited(): pl.pallas_call(functools.partial(partner_kernel, spacing, group), out_sha...  2.36 us
    pallas_call x1, Pallas kernels, composited(): pl.pallas_call(functools.partial(own_kernel, spacing), out_shape=(f32(pla...  2.26 us
    unnamed x4, local copies, waits for them, and re-layouts  1.4 us
  transfers between devices with their start and end apart: 3, of which 1 were waited for; matrix products, arithmetic and copies ran while one was open for 0% of the time, Pallas kernels for 14%

profile of v5, /device:TPU:385, one launch (start us, length us, event | category | flops | bytes accessed | tf_op | source)
XLA Modules:
  0.0 43.9 jit_solution(12180326948386361987)
XLA Ops:
  0.0 2.6 %collective-permute-start = (f32[4,96,1024]{2,1,0:T(8,128)}, f32[4,96,1024]{2,1,0:T(8,128)S(1)}, u32[]{:S(2)}, u32[]{:S(2)}) collective-permute-start(f32[4,96,1024]{2,1,0:T(8,128)} %field.3), channel_id=1, source_target_pairs={{0,16},{16,0},{32,48},{48,32},{64,80},{80,64},{96,112},{112,96},{1... | collective-permute-start | bytes 4718600 | tf_op jit(solution)/shard_map/ppermute | solution.py:350
  2.6 0.0 copy-start
  2.6 1.4 %copy-done = f32[4,96,1024]{2,1,0:T(8,128)S(1)} copy-done((f32[4,96,1024]{2,1,0:T(8,128)S(1)}, f32[4,96,1024]{2,1,0:T(8,128)}, u32[]{:S(2)}) %copy-start) | copy-done | bytes 1572888
  4.0 0.0 copy-start.1
  4.0 0.2 fetch.1
  4.2 3.1 %collective-permute-start.1 = (f32[1,96,1024]{2,1,0:T(8,128)S(1)}, f32[1,96,1024]{2,1,0:T(8,128)S(1)}, u32[]{:S(2)}, u32[]{:S(2)}) collective-permute-start(f32[1,96,1024]{2,1,0:T(8,128)S(1)} %fetch.1), channel_id=1, source_target_pairs={{16,32},{48,64},{80,96},{112,128},{144,160},{176,192},{208,224},{2... | collective-permute-start | bytes 1179656 | tf_op jit(solution)/shard_map/ppermute | solution.py:345
  7.3 0.0 copy-done.1
  7.4 2.3 %own.1 = (f32[4,9,112,128]{3,2,1,0:T(8,128)S(1)}, f32[4,6,64,128]{3,2,1,0:T(8,128)S(1)}) custom-call(f32[4,96,1024]{2,1,0:T(8,128)S(1)} %copy-done.1), custom_call_target="tpu_custom_call" | custom-call | flops 67108864 | bytes 2097152 | tf_op jit(solution)/shard_map/own/pallas_call | solution.py:352
  9.6 3.8 %collective-permute-done.1.outer = f32[1,96,1024]{2,1,0:T(8,128)S(1)} collective-permute-done((f32[1,96,1024]{2,1,0:T(8,128)S(1)}, f32[1,96,1024]{2,1,0:T(8,128)S(1)}, u32[]{:S(2)}, u32[]{:S(2)}) %collective-permute-start.1) | collective-permute-done | bytes 393248 | tf_op jit(solution)/shard_map/ppermute | solution.py:345
  13.4 0.0 collective-permute-done.partner
  13.4 0.1 edges.1
  13.5 3.8 %collective-permute-start.2 = (f32[72,128]{1,0:T(8,128)S(1)}, f32[72,128]{1,0:T(8,128)S(1)}, u32[]{:S(2)}, u32[]{:S(2)}) collective-permute-start(f32[72,128]{1,0:T(8,128)S(1)} %get-tuple-element.14), channel_id=1, source_target_pairs={{0,1},{1,2},{2,3},{3,4},{4,5},{5,6},{6,7},{7,8},{8,9},{9,10},{10,1... | collective-permute-start | bytes 110600 | tf_op jit(solution)/shard_map/ppermute | solution.py:374
  17.4 1.2 %shard_map.18.sums1 = f32[4,3,64,128]{3,2,1,0:T(8,128)S(1)} custom-call(f32[4,9,112,128]{3,2,1,0:T(8,128)S(1)} %get-tuple-element.10.own, f32[4,96,1024]{2,1,0:T(8,128)S(1)} %collective-permute-done.partner, f32[4,6,64,128]{3,2,1,0:T(8,128)S(1)} %get-tuple-element.11.own_sums), custom_call_target="tpu_custom_call" | custom-call | flops 33554432 | bytes 1048576 | tf_op jit(solution)/shard_map/pallas_call | solution.py:384
  18.6 1.2 %shard_map.17.sums0 = f32[4,3,64,128]{3,2,1,0:T(8,128)S(1)} custom-call(f32[4,9,112,128]{3,2,1,0:T(8,128)S(1)} %get-tuple-element.10.own, f32[4,96,1024]{2,1,0:T(8,128)S(1)} %collective-permute-done.partner, f32[4,6,64,128]{3,2,1,0:T(8,128)S(1)} %get-tuple-element.11.own_sums), custom_call_target="tpu_custom_call" | custom-call | flops 33554432 | bytes 1048576 | tf_op jit(solution)/shard_map/pallas_call | solution.py:384
  19.8 1.2 %outer.1.main = f32[1536,128]{1,0:T(8,128)S(1)} custom-call(f32[4,3,64,128]{3,2,1,0:T(8,128)S(1)} %shard_map.17.sums0, f32[4,3,64,128]{3,2,1,0:T(8,128)S(1)} %shard_map.18.sums1, f32[4,9,112,128]{3,2,1,0:T(8,128)S(1)} %get-tuple-element.10.own, f32[1,96,1024]{2,1,0:T(8,128)S(1)} %collective-permute-done.1.outer), custom_call_target="tpu_custom_call" | custom-call | flops 16777216 | bytes 2097152 | tf_op jit(solution)/shard_map/outer/pallas_call | solution.py:394
  21.0 0.0 collective-permute-done.2.beside
  21.0 0.1 line.1
  21.2 22.0 %all_to_all.5 = f32[16,96,128]{2,1,0:T(8,128)S(1)} all-to-all(f32[16,96,128]{2,1,0:T(8,128)S(1)} %bitcast.3), channel_id=1, replica_groups={{0,32,64,96,128,160,192,224,256,288,320,352,384,416,448,480},{16,48,80,..., dimensions={0} | all-to-all | bytes 1572864 | tf_op jit(solution)/shard_map/all_to_all | solution.py:415
  43.2 0.7 %blend.1 = f32[3,4,1024]{2,1,0:T(4,128)} custom-call(f32[1536,128]{1,0:T(8,128)S(1)} %bitcast.4), custom_call_target="tpu_custom_call" | custom-call | tf_op jit(solution)/shard_map/blend/pallas_call | solution.py:423
Async XLA Ops:
  0.0 13.4 %collective-permute-start = (f32[4,96,1024]{2,1,0:T(8,128)}, f32[4,96,1024]{2,1,0:T(8,128)S(1)}, u32[]{:S(2)}, u32[]{:S(2)}) collective-permute-start(f32[4,96,1024]{2,1,0:T(8,128)} %field.3), channel_id=1, source_target_pairs={{0,16},{16,0},{32,48},{48,32},{64,80},{80,64},{96,112},{112,96},{1... | collective-permute-start | bytes 4718600 | tf_op jit(solution)/shard_map/ppermute | solution.py:350
  2.6 1.4 %copy-start = (f32[4,96,1024]{2,1,0:T(8,128)S(1)}, f32[4,96,1024]{2,1,0:T(8,128)}, u32[]{:S(2)}) copy-start(f32[4,96,1024]{2,1,0:T(8,128)} %field.3) | copy-start | bytes 4718596
  4.0 3.4 %copy-start.1 = (f32[4,96,1024]{2,1,0:T(8,128)S(1)}, f32[4,96,1024]{2,1,0:T(8,128)}, u32[]{:S(2)}) copy-start(f32[4,96,1024]{2,1,0:T(8,128)} %field.3) | copy-start | bytes 4718596
  4.2 9.2 %collective-permute-start.1 = (f32[1,96,1024]{2,1,0:T(8,128)S(1)}, f32[1,96,1024]{2,1,0:T(8,128)S(1)}, u32[]{:S(2)}, u32[]{:S(2)}) collective-permute-start(f32[1,96,1024]{2,1,0:T(8,128)S(1)} %fetch.1), channel_id=1, source_target_pairs={{16,32},{48,64},{80,96},{112,128},{144,160},{176,192},{208,224},{2... | collective-permute-start | bytes 1179656 | tf_op jit(solution)/shard_map/ppermute | solution.py:345
  13.5 7.5 %collective-permute-start.2 = (f32[72,128]{1,0:T(8,128)S(1)}, f32[72,128]{1,0:T(8,128)S(1)}, u32[]{:S(2)}, u32[]{:S(2)}) collective-permute-start(f32[72,128]{1,0:T(8,128)S(1)} %get-tuple-element.14), channel_id=1, source_target_pairs={{0,1},{1,2},{2,3},{3,4},{4,5},{5,6},{6,7},{7,8},{8,9},{9,10},{10,1... | collective-permute-start | bytes 110600 | tf_op jit(solution)/shard_map/ppermute | solution.py:374

commit v6 on v5

--- a/solution.py
+++ b/solution.py
@@ -19,29 +19,30 @@
 
 LANES = 128
 LOG2E = math.log2(math.e)
+SHINE = 0.7 * light_cols
 FIRST = 8
 PITCH = 112
 VMEM = pl.BlockSpec(memory_space=pltpu.VMEM)
 
 
-def sample_step(spacing, state, low, high, half, above, below, slope_cols):
+def sample_step(spacing, state, low, high, twice, above, below, columns):
     run, through, total, tilt, middle = state
     run = run - spacing * LOG2E * floor_density
     for centre, spread, bump in zip(centres, spreads, heights):
-        offset = half - 0.5 * centre
+        offset = twice - 2.0 * centre
         run = run - jnp.exp2(
-            (offset * offset) * (-4.0 * LOG2E / (spread * spread)) + math.log2(bump * spacing * LOG2E)
+            (offset * offset) * (-0.25 * LOG2E / (spread * spread)) + math.log2(bump * spacing * LOG2E)
         )
     now = jnp.exp2(run)
     weight = through - now
-    slope_rows = below - above
-    slope_depth = high - low
-    facing = (0.7 * light_cols) * slope_cols + (0.7 * light_rows) * slope_rows + (0.7 * light_depth) * slope_depth
-    length = slope_cols * slope_cols + slope_rows * slope_rows + slope_depth * slope_depth + 1.0
-    lit = weight * (0.3 + jnp.abs(facing) * lax.rsqrt(length))
+    rise = below - above
+    depth = high - low
+    facing = columns + (light_rows / light_cols) * rise + (4.0 * light_depth / light_cols) * depth
+    length = columns * columns + rise * rise + (16.0 * (depth * depth) + 16.0)
+    lit = weight * (0.3 / SHINE + jnp.abs(facing) * lax.rsqrt(length))
     total = total + lit
-    tilt = tilt + lit * jnp.tanh(2.0 * half)
-    middle = middle + lit * jnp.exp2((half * half) * (-4.0 * LOG2E))
+    tilt = tilt + lit * jnp.tanh(0.5 * twice)
+    middle = middle + lit * jnp.exp2((twice * twice) * (-0.25 * LOG2E))
     return run, now, total, tilt, middle
 
 
@@ -132,17 +133,17 @@
         else:
             high = [picked(plane + 1, tile, group, offset) for offset in range(-1, 4)]
             high_cols = plane_differences(picked, plane + 1, tile, tiles, group, high[1:4])
-        half = [0.25 * (a + b) for a, b in zip(low, high)]
+        twice = [a + b for a, b in zip(low, high)]
         for row in range(3):
             states[row] = sample_step(
                 spacing,
                 states[row],
                 low[row + 1],
                 high[row + 1],
-                half[row + 1],
-                half[row],
-                half[row + 2],
-                0.25 * (low_cols[row] + high_cols[row]),
+                twice[row + 1],
+                twice[row],
+                twice[row + 2],
+                low_cols[row] + high_cols[row],
             )
         low, low_cols = high, high_cols
     return states
@@ -172,14 +173,15 @@
         copy.wait()
     picked = picker(own, core_index())
 
-    def step(index, carry):
-        group, tile = index // tiles, lax.rem(index, tiles)
-        for row, state in enumerate(shade_tile(spacing, picked, range(planes - 1), tile, tiles, group)):
-            for n, value in enumerate(state[1:]):
-                sums[n, group * 3 + row, pl.ds(tile * 8, 8), :] = value
+    def step(tile, carry):
+        part = pl.ds(tile * 8, 8)
+        for group in range(sums.shape[1] // 3):
+            for row, state in enumerate(shade_tile(spacing, picked, range(planes - 1), tile, tiles, group)):
+                for n, value in enumerate(state[1:]):
+                    sums[n, group * 3 + row, part, :] = value
         return carry
 
-    lax.fori_loop(0, sums.shape[1] // 3 * tiles, step, 0)
+    lax.fori_loop(0, tiles, step, 0)
 
 
 def partner_kernel(spacing, group, own, partner, own_sums, sums, buf):
@@ -196,15 +198,16 @@
     buf[:, tiles, :, :] = jnp.zeros((planes + 1, PITCH, LANES), jnp.float32)
     picked = picker(buf, core)
 
-    def step(tile, carry):
-        part = pl.ds(tile * 8, 8)
-        for row, state in enumerate(shade_tile(spacing, picked, range(planes), tile, tiles, group)):
-            nearer = tuple(own_sums[n, group * 3 + row, part, :] for n in range(4))
-            for n, value in enumerate(join(core == 0, nearer, state[1:])):
-                sums[n, row, part, :] = value
+    def step(pair, carry):
+        for tile in (2 * pair, 2 * pair + 1):
+            part = pl.ds(tile * 8, 8)
+            for row, state in enumerate(shade_tile(spacing, picked, range(planes), tile, tiles, group)):
+                nearer = tuple(own_sums[n, group * 3 + row, part, :] for n in range(4))
+                for n, value in enumerate(join(core == 0, nearer, state[1:])):
+                    sums[n, row, part, :] = value
         return carry
 
-    lax.fori_loop(0, tiles, step, 0)
+    lax.fori_loop(0, tiles // 2, step, 0)
 
     @pl.when(lax.axis_index("depth") == lax.axis_size("depth") - 2)
     def _():
@@ -223,7 +226,7 @@
 def finished(core, present, bulk, outer):
     outer = (jnp.where(present, outer[0], 1.0), *[jnp.where(present, value, 0.0) for value in outer[1:]])
     through, total, tilt, middle = join(core == 1, bulk, outer)
-    return 0.5 * (total + tilt), middle, 0.5 * (total - tilt), through
+    return (0.5 * SHINE) * (total + tilt), SHINE * middle, (0.5 * SHINE) * (total - tilt), through
 
 
 def outer_kernel(spacing, sums0, sums1, own, outer, out, buf):
@@ -245,17 +248,17 @@
             far = [far_picked(0, tile, group, offset) for offset in range(-1, 4)]
             near_cols = plane_differences(near_picked, nearest, tile, tiles, group, near[1:4])
             far_cols = plane_differences(far_picked, 0, tile, tiles, group, far[1:4])
-            half = [0.25 * (a + b) for a, b in zip(near, far)]
+            twice = [a + b for a, b in zip(near, far)]
             for row in range(3):
                 sample = sample_step(
                     spacing,
                     start_state(),
                     to_high * near[row + 1],
                     to_high * far[row + 1],
-                    half[row + 1],
-                    half[row],
-                    half[row + 2],
-                    0.25 * (near_cols[row] + far_cols[row]),
+                    twice[row + 1],
+                    twice[row],
+                    twice[row + 2],
+                    near_cols[row] + far_cols[row],
                 )
                 bulk = tuple(sums[n, row, part, :] for n in range(4))
                 for channel, value in enumerate(finished(core, present, bulk, sample[1:])):
@@ -276,10 +279,10 @@
         return edge[at, :], inner[at, :], beside[at, :]
 
     def line_step(line, low, high):
-        half, within, beyond = [0.25 * (a + b) for a, b in zip(low, high)]
+        twice, within, beyond = [a + b for a, b in zip(low, high)]
         above = jnp.where(core == 0, beyond, within)
         below = jnp.where(core == 0, within, beyond)
-        return sample_step(spacing, line, low[0], high[0], half, above, below, row_slopes(half))
+        return sample_step(spacing, line, low[0], high[0], twice, above, below, row_slopes(twice))
 
     line = start_state()
     for plane in range(planes - 1):

time: 44.1 us -> 44.1 us (level)
  the two profiles are of different devices: /device:TPU:385 before, /device:TPU:353 now
where the time goes in v6:
time: 44.1 us; the launch traced here: 43.9 us
  blocking collectives  23.6 us (54%)
  starting transfers between devices  8.36 us (19%)
  Pallas kernels  5.71 us (13%)
  waiting for transfers between devices  4.72 us (11%)
  local copies, waits for them, and re-layouts  1.4 us (3%)
    all_to_all x1, blocking collectives, composited(): lax.all_to_all(parts.reshape(chips, 96, LANES), 'depth', split_axis=0, co...  23.6 us
    ppermute x1, waiting for transfers between devices, composited(): lax.ppermute(outer_out, 'depth', [(2 * k + 1, 2 * k + 2) for k in range(c...  4.55 us
    ppermute x1, starting transfers between devices, composited(): lax.ppermute(outer_out, 'depth', [(2 * k + 1, 2 * k + 2) for k in range(c...  3.15 us
    ppermute x1, starting transfers between devices, composited(): lax.ppermute(sent, ('depth', 'tile'), [(place(2 * k, t), place(2 * k, t +...  2.64 us
    ppermute x1, starting transfers between devices, composited(): partner = lax.ppermute(field, 'depth', [(i, i ^ 1) for i in range(depth)])  2.57 us
    pallas_call x2, Pallas kernels, composited(): pl.pallas_call(functools.partial(partner_kernel, spacing, group), out_sha...  1.86 us
    pallas_call x1, Pallas kernels, composited(): pl.pallas_call(functools.partial(own_kernel, spacing), out_shape=(f32(pla...  1.51 us
    unnamed x4, local copies, waits for them, and re-layouts  1.4 us
  transfers between devices with their start and end apart: 3, of which 2 were waited for; matrix products, arithmetic and copies ran while one was open for 0% of the time, Pallas kernels for 11%

profile of v6, /device:TPU:353, one launch (start us, length us, event | category | flops | bytes accessed | tf_op | source)
XLA Modules:
  0.0 43.9 jit_solution(1022028899001369903)
XLA Ops:
  0.0 2.6 %collective-permute-start = (f32[4,96,1024]{2,1,0:T(8,128)}, f32[4,96,1024]{2,1,0:T(8,128)S(1)}, u32[]{:S(2)}, u32[]{:S(2)}) collective-permute-start(f32[4,96,1024]{2,1,0:T(8,128)} %field.3), channel_id=1, source_target_pairs={{0,16},{16,0},{32,48},{48,32},{64,80},{80,64},{96,112},{112,96},{1... | collective-permute-start | bytes 4718600 | tf_op jit(solution)/shard_map/ppermute | solution.py:353
  2.6 0.0 copy-start
  2.6 1.4 %copy-done = f32[4,96,1024]{2,1,0:T(8,128)S(1)} copy-done((f32[4,96,1024]{2,1,0:T(8,128)S(1)}, f32[4,96,1024]{2,1,0:T(8,128)}, u32[]{:S(2)}) %copy-start) | copy-done | bytes 1572888
  4.0 0.0 copy-start.1
  4.0 0.2 fetch.1
  4.2 3.1 %collective-permute-start.1 = (f32[1,96,1024]{2,1,0:T(8,128)S(1)}, f32[1,96,1024]{2,1,0:T(8,128)S(1)}, u32[]{:S(2)}, u32[]{:S(2)}) collective-permute-start(f32[1,96,1024]{2,1,0:T(8,128)S(1)} %fetch.1), channel_id=1, source_target_pairs={{16,32},{48,64},{80,96},{112,128},{144,160},{176,192},{208,224},{2... | collective-permute-start | bytes 1179656 | tf_op jit(solution)/shard_map/ppermute | solution.py:348
  7.3 0.0 copy-done.1
  7.4 1.5 %own.1 = (f32[4,9,112,128]{3,2,1,0:T(8,128)S(1)}, f32[4,6,64,128]{3,2,1,0:T(8,128)S(1)}) custom-call(f32[4,96,1024]{2,1,0:T(8,128)S(1)} %copy-done.1), custom_call_target="tpu_custom_call" | custom-call | flops 67108864 | bytes 2097152 | tf_op jit(solution)/shard_map/own/pallas_call | solution.py:355
  8.9 4.5 %collective-permute-done.1.outer = f32[1,96,1024]{2,1,0:T(8,128)S(1)} collective-permute-done((f32[1,96,1024]{2,1,0:T(8,128)S(1)}, f32[1,96,1024]{2,1,0:T(8,128)S(1)}, u32[]{:S(2)}, u32[]{:S(2)}) %collective-permute-start.1) | collective-permute-done | bytes 393248 | tf_op jit(solution)/shard_map/ppermute | solution.py:348
  13.4 0.0 collective-permute-done.partner
  13.4 0.1 edges.1
  13.5 2.6 %collective-permute-start.2 = (f32[72,128]{1,0:T(8,128)S(1)}, f32[72,128]{1,0:T(8,128)S(1)}, u32[]{:S(2)}, u32[]{:S(2)}) collective-permute-start(f32[72,128]{1,0:T(8,128)S(1)} %get-tuple-element.14), channel_id=1, source_target_pairs={{0,1},{1,2},{2,3},{3,4},{4,5},{5,6},{6,7},{7,8},{8,9},{9,10},{10,1... | collective-permute-start | bytes 110600 | tf_op jit(solution)/shard_map/ppermute | solution.py:377
  16.2 0.9 %shard_map.18.sums1 = f32[4,3,64,128]{3,2,1,0:T(8,128)S(1)} custom-call(f32[4,9,112,128]{3,2,1,0:T(8,128)S(1)} %get-tuple-element.10.own, f32[4,96,1024]{2,1,0:T(8,128)S(1)} %collective-permute-done.partner, f32[4,6,64,128]{3,2,1,0:T(8,128)S(1)} %get-tuple-element.11.own_sums), custom_call_target="tpu_custom_call" | custom-call | flops 33554432 | bytes 1048576 | tf_op jit(solution)/shard_map/pallas_call | solution.py:387
  17.1 0.9 %shard_map.17.sums0 = f32[4,3,64,128]{3,2,1,0:T(8,128)S(1)} custom-call(f32[4,9,112,128]{3,2,1,0:T(8,128)S(1)} %get-tuple-element.10.own, f32[4,96,1024]{2,1,0:T(8,128)S(1)} %collective-permute-done.partner, f32[4,6,64,128]{3,2,1,0:T(8,128)S(1)} %get-tuple-element.11.own_sums), custom_call_target="tpu_custom_call" | custom-call | flops 33554432 | bytes 1048576 | tf_op jit(solution)/shard_map/pallas_call | solution.py:387
  18.0 1.2 %outer.1.main = f32[1536,128]{1,0:T(8,128)S(1)} custom-call(f32[4,3,64,128]{3,2,1,0:T(8,128)S(1)} %shard_map.17.sums0, f32[4,3,64,128]{3,2,1,0:T(8,128)S(1)} %shard_map.18.sums1, f32[4,9,112,128]{3,2,1,0:T(8,128)S(1)} %get-tuple-element.10.own, f32[1,96,1024]{2,1,0:T(8,128)S(1)} %collective-permute-done.1.outer), custom_call_target="tpu_custom_call" | custom-call | flops 16777216 | bytes 2097152 | tf_op jit(solution)/shard_map/outer/pallas_call | solution.py:397
  19.3 0.2 collective-permute-done.2.beside
  19.4 0.1 line.1
  19.6 23.6 %all_to_all.5 = f32[16,96,128]{2,1,0:T(8,128)S(1)} all-to-all(f32[16,96,128]{2,1,0:T(8,128)S(1)} %bitcast.3), channel_id=1, replica_groups={{0,32,64,96,128,160,192,224,256,288,320,352,384,416,448,480},{16,48,80,..., dimensions={0} | all-to-all | bytes 1572864 | tf_op jit(solution)/shard_map/all_to_all | solution.py:418
  43.2 0.7 %blend.1 = f32[3,4,1024]{2,1,0:T(4,128)} custom-call(f32[1536,128]{1,0:T(8,128)S(1)} %bitcast.4), custom_call_target="tpu_custom_call" | custom-call | tf_op jit(solution)/shard_map/blend/pallas_call | solution.py:426
Async XLA Ops:
  0.0 13.4 %collective-permute-start = (f32[4,96,1024]{2,1,0:T(8,128)}, f32[4,96,1024]{2,1,0:T(8,128)S(1)}, u32[]{:S(2)}, u32[]{:S(2)}) collective-permute-start(f32[4,96,1024]{2,1,0:T(8,128)} %field.3), channel_id=1, source_target_pairs={{0,16},{16,0},{32,48},{48,32},{64,80},{80,64},{96,112},{112,96},{1... | collective-permute-start | bytes 4718600 | tf_op jit(solution)/shard_map/ppermute | solution.py:353
  2.6 1.4 %copy-start = (f32[4,96,1024]{2,1,0:T(8,128)S(1)}, f32[4,96,1024]{2,1,0:T(8,128)}, u32[]{:S(2)}) copy-start(f32[4,96,1024]{2,1,0:T(8,128)} %field.3) | copy-start | bytes 4718596
  4.0 3.4 %copy-start.1 = (f32[4,96,1024]{2,1,0:T(8,128)S(1)}, f32[4,96,1024]{2,1,0:T(8,128)}, u32[]{:S(2)}) copy-start(f32[4,96,1024]{2,1,0:T(8,128)} %field.3) | copy-start | bytes 4718596
  4.2 9.2 %collective-permute-start.1 = (f32[1,96,1024]{2,1,0:T(8,128)S(1)}, f32[1,96,1024]{2,1,0:T(8,128)S(1)}, u32[]{:S(2)}, u32[]{:S(2)}) collective-permute-start(f32[1,96,1024]{2,1,0:T(8,128)S(1)} %fetch.1), channel_id=1, source_target_pairs={{16,32},{48,64},{80,96},{112,128},{144,160},{176,192},{208,224},{2... | collective-permute-start | bytes 1179656 | tf_op jit(solution)/shard_map/ppermute | solution.py:348
  13.5 5.9 %collective-permute-start.2 = (f32[72,128]{1,0:T(8,128)S(1)}, f32[72,128]{1,0:T(8,128)S(1)}, u32[]{:S(2)}, u32[]{:S(2)}) collective-permute-start(f32[72,128]{1,0:T(8,128)S(1)} %get-tuple-element.14), channel_id=1, source_target_pairs={{0,1},{1,2},{2,3},{3,4},{4,5},{5,6},{6,7},{7,8},{8,9},{9,10},{10,1... | collective-permute-start | bytes 110600 | tf_op jit(solution)/shard_map/ppermute | solution.py:377

commit v7 on v6

--- a/solution.py
+++ b/solution.py
@@ -22,6 +22,7 @@
 SHINE = 0.7 * light_cols
 FIRST = 8
 PITCH = 112
+OUTER_ROWS = 80
 VMEM = pl.BlockSpec(memory_space=pltpu.VMEM)
 
 
@@ -65,10 +66,34 @@
     return lax.rem(lax.axis_index("depth"), 2)
 
 
-def fetch_kernel(field, outer, sem):
-    copy = pltpu.make_async_copy(field.at[pl.ds((field.shape[0] - 1) * core_index(), 1)], outer, sem)
-    copy.start()
-    copy.wait()
+def fetch_kernel(field, outer, plane, sems):
+    planes, rows, width = field.shape
+    core = core_index()
+    copies = [
+        pltpu.make_async_copy(
+            field.at[(planes - 1) * core, :, pl.ds(tile * LANES, LANES)],
+            plane.at[0, tile, pl.ds(FIRST, rows), :],
+            sems.at[tile],
+        )
+        for tile in range(width // LANES)
+    ]
+    for copy in copies:
+        copy.start()
+    for copy in copies:
+        copy.wait()
+    picked = picker(plane, 1 - core)
+    for tile in range(width // LANES):
+        for offset in range(-1, 4):
+            for group in range(2):
+                outer[outer_row(tile, group, offset), :] = picked(0, tile, group, offset)
+        at = OUTER_ROWS * (width // LANES) + tile
+        outer[at : at + 1, :] = jnp.where(
+            core == 1, plane[0, tile, FIRST + rows - 1 : FIRST + rows, :], plane[0, tile, FIRST : FIRST + 1, :]
+        )
+
+
+def outer_row(tile, group, offset):
+    return pl.ds(pl.multiple_of(tile * OUTER_ROWS, 8) + (offset + 1) * 16 + group * 8, 8)
 
 
 def edge_kernel(own, partner, outer, sent, edge, inner):
@@ -85,7 +110,11 @@
             return partner[slot, at : at + 1, lanes]
 
         def beyond(slot, at):
-            return outer[0, at : at + 1, lanes]
+            if n == rows - 1:
+                at = OUTER_ROWS * (width // LANES) + tile
+            else:
+                at = tile * OUTER_ROWS + (16 * (at + 1) if at < 8 else 16 * (at + 1 - (rows - 3)) + 15)
+            return outer[at : at + 1, :]
 
         if plane == 2 * planes:
             at_core0 = at_core1 = beyond
@@ -211,16 +240,17 @@
 
     @pl.when(lax.axis_index("depth") == lax.axis_size("depth") - 2)
     def _():
-        def last_step(tile, carry):
-            part = pl.ds(tile * 8, 8)
-            last = range(planes, planes + 1)
-            for row, state in enumerate(shade_tile(spacing, picked, last, tile, tiles, group, last=True)):
-                nearer = tuple(sums[n, row, part, :] for n in range(4))
-                for n, value in enumerate(join(True, nearer, state[1:])):
-                    sums[n, row, part, :] = value
+        def last_step(turn, carry):
+            for tile in [4 * turn + n for n in range(4)]:
+                part = pl.ds(tile * 8, 8)
+                last = range(planes, planes + 1)
+                for row, state in enumerate(shade_tile(spacing, picked, last, tile, tiles, group, last=True)):
+                    nearer = tuple(sums[n, row, part, :] for n in range(4))
+                    for n, value in enumerate(join(True, nearer, state[1:])):
+                        sums[n, row, part, :] = value
             return carry
 
-        lax.fori_loop(0, tiles, last_step, 0)
+        lax.fori_loop(0, tiles // 4, last_step, 0)
 
 
 def finished(core, present, bulk, outer):
@@ -231,14 +261,16 @@
 
 def outer_kernel(spacing, sums0, sums1, own, outer, out, buf):
     slots, tiles = own.shape[0], own.shape[1] - 1
-    rows = outer.shape[1]
     core = core_index()
     present = lax.axis_index("depth") != 0
-    for tile in range(tiles):
-        buf[0, tile, FIRST : FIRST + rows, :] = outer[0, :, tile * LANES : (tile + 1) * LANES]
-    buf[:, tiles, :, :] = jnp.zeros((1, PITCH, LANES), jnp.float32)
+    buf[0 : tiles * OUTER_ROWS, :] = outer[0 : tiles * OUTER_ROWS, :]
+    buf[tiles * OUTER_ROWS :, :] = jnp.zeros((OUTER_ROWS, LANES), jnp.float32)
     to_high = jnp.where(core == 0, -1.0, 1.0)
-    near_picked, far_picked = picker(own, core), picker(buf, core)
+    near_picked = picker(own, core)
+
+    def far_picked(plane, tile, group, offset):
+        return buf[outer_row(tile, group, offset), :]
+
     nearest = (slots - 1) * core
 
     def shade(tile, carry):
@@ -337,10 +369,10 @@
 
     outer_out = pl.pallas_call(
         fetch_kernel,
-        out_shape=f32(1, rows, width),
+        out_shape=f32((OUTER_ROWS + 1) * tiles, LANES),
         in_specs=[pl.BlockSpec(memory_space=pltpu.HBM)],
         out_specs=VMEM,
-        scratch_shapes=[pltpu.SemaphoreType.DMA],
+        scratch_shapes=[pltpu.VMEM((1, tiles, PITCH, LANES), jnp.float32), pltpu.SemaphoreType.DMA((tiles,))],
         compiler_params=pltpu.CompilerParams(vmem_limit_bytes=4 << 20),
         cost_estimate=cost(1 << 10, 1 << 20),
         name="fetch",
@@ -399,7 +431,7 @@
         out_shape=f32(chips * 96, LANES),
         in_specs=[VMEM] * 4,
         out_specs=VMEM,
-        scratch_shapes=[pltpu.VMEM((1, tiles + 1, PITCH, LANES), jnp.float32)],
+        scratch_shapes=[pltpu.VMEM(((tiles + 1) * OUTER_ROWS, LANES), jnp.float32)],
         compiler_params=pltpu.CompilerParams(vmem_limit_bytes=12 << 20),
         cost_estimate=cost(1 << 24, 1 << 21),
         name="outer",

time: 44.1 us -> 43 us (0.975)
  the two profiles are of different devices: /device:TPU:353 before, /device:TPU:96 now
where the time goes in v7:
time: 43 us; the launch traced here: 42.8 us
  blocking collectives  27.4 us (64%)
  starting transfers between devices  7.76 us (18%)
  Pallas kernels  5.67 us (13%)
  local copies, waits for them, and re-layouts  1.81 us (4%)
    all_to_all x1, blocking collectives, composited(): lax.all_to_all(parts.reshape(chips, 96, LANES), 'depth', split_axis=0, co...  27.4 us
    ppermute x1, starting transfers between devices, composited(): lax.ppermute(sent, ('depth', 'tile'), [(place(2 * k, t), place(2 * k, t +...  5.04 us
    ppermute x1, starting transfers between devices, composited(): partner = lax.ppermute(field, 'depth', [(i, i ^ 1) for i in range(depth)])  1.91 us
    pallas_call x2, Pallas kernels, composited(): pl.pallas_call(functools.partial(partner_kernel, spacing, group), out_sha...  1.86 us
    unnamed x4, local copies, waits for them, and re-layouts  1.81 us
    pallas_call x1, Pallas kernels, composited(): pl.pallas_call(functools.partial(own_kernel, spacing), out_shape=(f32(pla...  1.5 us
    pallas_call x1, Pallas kernels, composited(): pl.pallas_call(functools.partial(outer_kernel, spacing), out_shape=f32(ch...  1.21 us
  transfers between devices with their start and end apart: 3, of which 0 were waited for; matrix products, arithmetic and copies ran while one was open for 0% of the time, Pallas kernels for 11%

profile of v7, /device:TPU:96, one launch (start us, length us, event | category | flops | bytes accessed | tf_op | source)
XLA Modules:
  0.0 42.8 jit_solution(7147932556488318800)
XLA Ops:
  0.0 1.9 %collective-permute-start = (f32[4,96,1024]{2,1,0:T(8,128)}, f32[4,96,1024]{2,1,0:T(8,128)S(1)}, u32[]{:S(2)}, u32[]{:S(2)}) collective-permute-start(f32[4,96,1024]{2,1,0:T(8,128)} %field.3), channel_id=1, source_target_pairs={{0,16},{16,0},{32,48},{48,32},{64,80},{80,64},{96,112},{112,96},{1... | collective-permute-start | bytes 4718600 | tf_op jit(solution)/shard_map/ppermute | solution.py:385
  1.9 0.0 copy-start
  1.9 1.4 %copy-done = f32[4,96,1024]{2,1,0:T(8,128)S(1)} copy-done((f32[4,96,1024]{2,1,0:T(8,128)S(1)}, f32[4,96,1024]{2,1,0:T(8,128)}, u32[]{:S(2)}) %copy-start) | copy-done | bytes 1572888
  3.3 0.0 copy-start.1
  3.3 0.2 fetch.1
  3.5 0.8 %collective-permute-start.1 = (f32[648,128]{1,0:T(8,128)S(1)}, f32[648,128]{1,0:T(8,128)S(1)}, u32[]{:S(2)}, u32[]{:S(2)}) collective-permute-start(f32[648,128]{1,0:T(8,128)S(1)} %fetch.1), channel_id=1, source_target_pairs={{16,32},{48,64},{80,96},{112,128},{144,160},{176,192},{208,224},{2... | collective-permute-start | bytes 995336 | tf_op jit(solution)/shard_map/ppermute | solution.py:380
  4.3 0.4 copy-done.1
  4.7 1.5 %own.1 = (f32[4,9,112,128]{3,2,1,0:T(8,128)S(1)}, f32[4,6,64,128]{3,2,1,0:T(8,128)S(1)}) custom-call(f32[4,96,1024]{2,1,0:T(8,128)S(1)} %copy-done.1), custom_call_target="tpu_custom_call" | custom-call | flops 67108864 | bytes 2097152 | tf_op jit(solution)/shard_map/own/pallas_call | solution.py:387
  6.2 0.0 collective-permute-done.1.outer
  6.3 0.0 collective-permute-done.partner
  6.3 0.1 edges.1
  6.4 5.0 %collective-permute-start.2 = (f32[72,128]{1,0:T(8,128)S(1)}, f32[72,128]{1,0:T(8,128)S(1)}, u32[]{:S(2)}, u32[]{:S(2)}) collective-permute-start(f32[72,128]{1,0:T(8,128)S(1)} %get-tuple-element.14), channel_id=1, source_target_pairs={{0,1},{1,2},{2,3},{3,4},{4,5},{5,6},{6,7},{7,8},{8,9},{9,10},{10,1... | collective-permute-start | bytes 110600 | tf_op jit(solution)/shard_map/ppermute | solution.py:409
  11.4 0.9 %shard_map.18.sums1 = f32[4,3,64,128]{3,2,1,0:T(8,128)S(1)} custom-call(f32[4,9,112,128]{3,2,1,0:T(8,128)S(1)} %get-tuple-element.10.own, f32[4,96,1024]{2,1,0:T(8,128)S(1)} %collective-permute-done.partner, f32[4,6,64,128]{3,2,1,0:T(8,128)S(1)} %get-tuple-element.11.own_sums), custom_call_target="tpu_custom_call" | custom-call | flops 33554432 | bytes 1048576 | tf_op jit(solution)/shard_map/pallas_call | solution.py:419
  12.4 0.9 %shard_map.17.sums0 = f32[4,3,64,128]{3,2,1,0:T(8,128)S(1)} custom-call(f32[4,9,112,128]{3,2,1,0:T(8,128)S(1)} %get-tuple-element.10.own, f32[4,96,1024]{2,1,0:T(8,128)S(1)} %collective-permute-done.partner, f32[4,6,64,128]{3,2,1,0:T(8,128)S(1)} %get-tuple-element.11.own_sums), custom_call_target="tpu_custom_call" | custom-call | flops 33554432 | bytes 1048576 | tf_op jit(solution)/shard_map/pallas_call | solution.py:419
  13.3 1.2 %outer.1.main = f32[1536,128]{1,0:T(8,128)S(1)} custom-call(f32[4,3,64,128]{3,2,1,0:T(8,128)S(1)} %shard_map.17.sums0, f32[4,3,64,128]{3,2,1,0:T(8,128)S(1)} %shard_map.18.sums1, f32[4,9,112,128]{3,2,1,0:T(8,128)S(1)} %get-tuple-element.10.own, f32[648,128]{1,0:T(8,128)S(1)} %collective-permute-done.1.outer), custom_call_target="tpu_custom_call" | custom-call | flops 16777216 | bytes 2097152 | tf_op jit(solution)/shard_map/outer/pallas_call | solution.py:429
  14.5 0.0 collective-permute-done.2.beside
  14.5 0.1 line.1
  14.7 27.4 %all_to_all.5 = f32[16,96,128]{2,1,0:T(8,128)S(1)} all-to-all(f32[16,96,128]{2,1,0:T(8,128)S(1)} %bitcast.3), channel_id=1, replica_groups={{0,32,64,96,128,160,192,224,256,288,320,352,384,416,448,480},{16,48,80,..., dimensions={0} | all-to-all | bytes 1572864 | tf_op jit(solution)/shard_map/all_to_all | solution.py:450
  42.1 0.7 %blend.1 = f32[3,4,1024]{2,1,0:T(4,128)} custom-call(f32[1536,128]{1,0:T(8,128)S(1)} %bitcast.4), custom_call_target="tpu_custom_call" | custom-call | tf_op jit(solution)/shard_map/blend/pallas_call | solution.py:458
Async XLA Ops:
  0.0 6.3 %collective-permute-start = (f32[4,96,1024]{2,1,0:T(8,128)}, f32[4,96,1024]{2,1,0:T(8,128)S(1)}, u32[]{:S(2)}, u32[]{:S(2)}) collective-permute-start(f32[4,96,1024]{2,1,0:T(8,128)} %field.3), channel_id=1, source_target_pairs={{0,16},{16,0},{32,48},{48,32},{64,80},{80,64},{96,112},{112,96},{1... | collective-permute-start | bytes 4718600 | tf_op jit(solution)/shard_map/ppermute | solution.py:385
  1.9 1.4 %copy-start = (f32[4,96,1024]{2,1,0:T(8,128)S(1)}, f32[4,96,1024]{2,1,0:T(8,128)}, u32[]{:S(2)}) copy-start(f32[4,96,1024]{2,1,0:T(8,128)} %field.3) | copy-start | bytes 4718596
  3.3 1.4 %copy-start.1 = (f32[4,96,1024]{2,1,0:T(8,128)S(1)}, f32[4,96,1024]{2,1,0:T(8,128)}, u32[]{:S(2)}) copy-start(f32[4,96,1024]{2,1,0:T(8,128)} %field.3) | copy-start | bytes 4718596
  3.5 2.7 %collective-permute-start.1 = (f32[648,128]{1,0:T(8,128)S(1)}, f32[648,128]{1,0:T(8,128)S(1)}, u32[]{:S(2)}, u32[]{:S(2)}) collective-permute-start(f32[648,128]{1,0:T(8,128)S(1)} %fetch.1), channel_id=1, source_target_pairs={{16,32},{48,64},{80,96},{112,128},{144,160},{176,192},{208,224},{2... | collective-permute-start | bytes 995336 | tf_op jit(solution)/shard_map/ppermute | solution.py:380
  6.4 8.1 %collective-permute-start.2 = (f32[72,128]{1,0:T(8,128)S(1)}, f32[72,128]{1,0:T(8,128)S(1)}, u32[]{:S(2)}, u32[]{:S(2)}) collective-permute-start(f32[72,128]{1,0:T(8,128)S(1)} %get-tuple-element.14), channel_id=1, source_target_pairs={{0,1},{1,2},{2,3},{3,4},{4,5},{5,6},{6,7},{7,8},{8,9},{9,10},{10,1... | collective-permute-start | bytes 110600 | tf_op jit(solution)/shard_map/ppermute | solution.py:409
